TPU v7x, 256 devices: a whole 4x4x8 slice. The times are simulated.
256 devices in a mesh: rows: 64 (over x, z, core), cols: 4 (over y).
Axes of the slice: x: 4, y: 4, z: 8, core: 2. Of those that a mesh axis runs over, the one named last changes fastest.
Arguments:
- leading_scene_data: float32 [2, 8192, 8192], P(None, 'rows', 'cols'), may hold values from -12 to 12, as said below
- trailing_scene_data: float32 [2, 8192, 8192], P(None, 'rows', 'cols'), may hold values from -20 to 20, as said below
- shared_usable_flags: int32 [8192, 8192], P('rows', 'cols'), may hold values 0 or 1
- sweep_of_each_line: int32 [8192], P('rows'), may hold values from 0 to 15, never falling along the last dimension, each value on 1 to 1024 neighbouring positions
Outputs:
- deramped: float32 [2, 8192, 8192], P(None, 'rows', 'cols')
- coherence: float32 [8192, 8192], P('rows', 'cols')
Inputs may be any that keep to these rules, and one draw needn't show every extreme that they name: `leading_scene_data`: first scene's parts lie in [-12, 12]. `trailing_scene_data`: second scene's parts lie in [-20, 20]; it is the first scene rotated by a smooth phase plus independent noise. `sweep_of_each_line`: burst ids never fall along the rows; each burst holds 1 to 1024 rows, one exactly that many.
All inputs are finite; a program needn't handle non-finite values.
Results may differ from a plain program's by a relative error of at most 0.0003.
Values sent between devices are 32-bit elements.
A program may use at most 64 MiB of HBM per device.

v0:
```python
import functools

import jax
import jax.numpy as jnp
from jax import lax
from jax.sharding import Mesh
from jax.sharding import PartitionSpec as P

WIN_R = 32
WIN_C = 8
SWEEP_TALLY = 16
ROWS = ("rows_0", "rows_1", "rows_2")
ROWS_COLS = ("rows_0", "rows_1", "rows_2", "cols")


largest_value = lax.Precision.HIGHEST


def extended(block, sides, width):
    for axis, dim in sides:
        count = lax.axis_size(axis)
        forward = [(i, i + 1) for i in range(count - 1)]
        backward = [(target, source) for source, target in forward]
        low = lax.ppermute(
            lax.slice_in_dim(block, block.shape[dim] - width, None, axis=dim), axis, forward
        )
        high = lax.ppermute(lax.slice_in_dim(block, 0, width, axis=dim), axis, backward)
        block = jnp.concatenate([low, block, high], axis=dim)
    return block


def by_axis(shard, axes):
    return functools.reduce(lax.psum, axes, shard)


def window_sum(planes, along_dim, length):
    offset = 1
    while offset < length:
        extent = planes.shape[along_dim]
        planes = lax.slice_in_dim(planes, 0, extent - offset, axis=along_dim) + lax.slice_in_dim(
            planes, offset, extent, axis=along_dim
        )
        offset = offset * 2
    return planes


def form_products(first_scene, second_scene, weight):
    real_a = first_scene[0] * weight
    imag_a = first_scene[1] * weight
    real_b = second_scene[0] * weight
    imag_b = second_scene[1] * weight
    return jnp.stack(
        [
            real_a * real_b + imag_a * imag_b,
            imag_a * real_b - real_a * imag_b,
            real_a * real_a + imag_a * imag_a,
            real_b * real_b + imag_b * imag_b,
        ]
    )


def sweep_aggregates(sweep_membership, line_aggregates):
    return jnp.dot(sweep_membership.T, line_aggregates, precision=largest_value)


def solve_ramps(pixel_count, moment_cc, moment_cr, moment_rr, sums):
    ridge_term = 0.001 * pixel_count + 1.0
    diag_col = moment_cc + ridge_term
    diag_row = moment_rr + ridge_term
    determinant = diag_col * diag_row - moment_cr * moment_cr
    base_part = sums[:, 0:2] / (pixel_count + ridge_term)[:, None]
    col_slope = (
        diag_row[:, None] * sums[:, 2:4] - moment_cr[:, None] * sums[:, 4:6]
    ) / determinant[:, None]
    row_slope = (
        diag_col[:, None] * sums[:, 4:6] - moment_cr[:, None] * sums[:, 2:4]
    ) / determinant[:, None]
    return jnp.concatenate([base_part, col_slope, row_slope], 1)


def on_device(leading_scene_data, trailing_scene_data, shared_usable_flags, sweep_of_each_line):
    rows_here, cols_here = shared_usable_flags.shape
    weight = shared_usable_flags.astype(jnp.float32)
    products = form_products(leading_scene_data, trailing_scene_data, weight)
    products = extended(products, ((ROWS, 1),), WIN_R // 2)
    products = extended(products, (("cols", 2),), WIN_C // 2)
    boxed = window_sum(window_sum(products, 1, WIN_R), 2, WIN_C)[:, :rows_here, :cols_here]
    normaliser = jnp.sqrt((boxed[2] + 1.0) * (boxed[3] + 1.0))
    coh_real = boxed[0] / normaliser
    coh_imag = boxed[1] / normaliser
    coherence = jnp.sqrt(coh_real * coh_real + coh_imag * coh_imag)
    total_rows = rows_here * lax.axis_size(ROWS)
    total_cols = cols_here * lax.axis_size("cols")
    row_first = (lax.axis_index(ROWS) * rows_here).astype(jnp.float32)
    col_first = (lax.axis_index("cols") * cols_here).astype(jnp.float32)
    along_coordinate = (row_first + jnp.arange(rows_here, dtype=jnp.float32) + 0.5) * (
        2.0 / total_rows
    ) - 1.0
    across_coordinate = (col_first + jnp.arange(cols_here, dtype=jnp.float32) + 0.5) * (
        2.0 / total_cols
    ) - 1.0
    sweep_membership = (
        sweep_of_each_line[:, None] == jnp.arange(SWEEP_TALLY, dtype=jnp.int32)[None, :]
    ).astype(jnp.float32)
    line_usable_tally = jnp.sum(weight, 1)
    along_across_moment = jnp.sum(weight * across_coordinate[None, :], 1)
    weighted_real = weight * coh_real
    weighted_imag = weight * coh_imag
    line_cross_inphase = jnp.sum(weighted_real, 1)
    line_cross_quadrature = jnp.sum(weighted_imag, 1)
    along_coordinate_power_two = jnp.sum(
        weight * across_coordinate[None, :] * across_coordinate[None, :], 1
    )
    along_weighted_inphase = jnp.sum(weighted_real * across_coordinate[None, :], 1)
    along_weighted_quadrature = jnp.sum(weighted_imag * across_coordinate[None, :], 1)
    moment_table = by_axis(
        sweep_aggregates(
            sweep_membership,
            jnp.stack(
                [
                    line_usable_tally,
                    along_across_moment,
                    along_coordinate * line_usable_tally,
                    along_coordinate_power_two,
                    along_coordinate * along_across_moment,
                    along_coordinate * along_coordinate * line_usable_tally,
                    line_cross_inphase,
                    line_cross_quadrature,
                    along_weighted_inphase,
                    along_weighted_quadrature,
                    along_coordinate * line_cross_inphase,
                    along_coordinate * line_cross_quadrature,
                ],
                1,
            ),
        ),
        ROWS_COLS,
    )
    pixel_count = moment_table[:, 0]
    sum_col = moment_table[:, 1]
    sum_row = moment_table[:, 2]
    floored = jnp.maximum(pixel_count, 1.0)
    middle_across = sum_col / floored
    middle_along = sum_row / floored
    moment_cc = (
        moment_table[:, 3]
        - 2.0 * middle_across * sum_col
        + middle_across * middle_across * pixel_count
    )
    moment_cr = (
        moment_table[:, 4]
        - middle_across * sum_row
        - middle_along * sum_col
        + middle_across * middle_along * pixel_count
    )
    moment_rr = (
        moment_table[:, 5]
        - 2.0 * middle_along * sum_row
        + middle_along * middle_along * pixel_count
    )
    base_sums = moment_table[:, 6:8]
    sums = jnp.concatenate(
        [
            base_sums,
            moment_table[:, 8:10] - middle_across[:, None] * base_sums,
            moment_table[:, 10:12] - middle_along[:, None] * base_sums,
        ],
        1,
    )
    along_displacement = along_coordinate - jnp.dot(
        sweep_membership, middle_along, precision=largest_value
    )
    across_displacement = (
        across_coordinate[None, :]
        - jnp.dot(sweep_membership, middle_across, precision=largest_value)[:, None]
    )
    planar_trends = solve_ramps(pixel_count, moment_cc, moment_cr, moment_rr, sums)
    for_each_line = jnp.dot(sweep_membership, planar_trends, precision=largest_value)
    model_real = (
        for_each_line[:, 0:1]
        + for_each_line[:, 2:3] * across_displacement
        + (for_each_line[:, 4] * along_displacement)[:, None]
    )
    model_imag = (
        for_each_line[:, 1:2]
        + for_each_line[:, 3:4] * across_displacement
        + (for_each_line[:, 5] * along_displacement)[:, None]
    )
    out_real = coh_real * model_real + coh_imag * model_imag
    out_imag = coh_imag * model_real - coh_real * model_imag
    return (jnp.stack([out_real, out_imag]), coherence)


def solution(mesh):
    finer = Mesh(
        mesh.devices.reshape(4, 8, 2, mesh.shape["cols"]), ("rows_0", "rows_1", "rows_2", "cols")
    )
    in_specs = (P(None, ROWS, "cols"), P(None, ROWS, "cols"), P(ROWS, "cols"), P(ROWS))
    out_specs = (P(None, ROWS, "cols"), P(ROWS, "cols"))
    return jax.shard_map(
        on_device, mesh=finer, in_specs=in_specs, out_specs=out_specs, check_vma=False
    )
```

profile of v0, /device:TPU:1, one launch (start us, length us, event | category | flops | bytes accessed | tf_op | source)
XLA Modules:
  0.0 103.6 jit_solution(6329575013122537683)
XLA Ops:
  0.6 3.2 %add_bitcast_fusion.2 = (f32[1,128,2048]{2,1,0:T(8,128)S(1)}, f32[1,128,2048]{2,1,0:T(8,128)S(1)}, f32[1,128,2048]{2,1,0:T(8,128)S(1)}, f32[1,128,2048]{2,1,0:T(8,128)S(1)}) fusion(s32[128,2048]{1,0:T(8,128)} %param.6, f32[2,128,2048]{2,1,0:T(8,128)} %param.4, f32[2,128,2048]{2,1,0:T(8,128)} %param.5), kind=kLoop, calls=%fused_computation.47 | loop fusion | flops 4456448 | bytes 9437184 | tf_op jit(solution)/shard_map/stack | solution.py:52
  3.9 0.0 copy-start.1
  3.9 1.0 copy-done.1
  4.8 1.0 pad_maximum_fusion.5
  5.9 4.9 %collective-permute-start = (f32[4,16,2048]{2,1,0:T(8,128)}, f32[4,16,2048]{2,1,0:T(8,128)}, u32[]{:S(2)}, u32[]{:S(2)}) collective-permute-start(f32[4,16,2048]{2,1,0:T(8,128)} %get-tuple-element.26), channel_id=1, source_target_pairs={{0,4},{4,8},{8,12},{12,16},{16,20},{20,24},{24,28},{28,32},{32,36}... | collective-permute-start | bytes 1572872 | tf_op jit(solution)/shard_map/ppermute | solution.py:24
  10.8 2.3 %collective-permute-start.1 = (f32[4,16,2048]{2,1,0:T(8,128)}, f32[4,16,2048]{2,1,0:T(8,128)}, u32[]{:S(2)}, u32[]{:S(2)}) collective-permute-start(f32[4,16,2048]{2,1,0:T(8,128)} %get-tuple-element.27), channel_id=1, source_target_pairs={{4,0},{8,4},{12,8},{16,12},{20,16},{24,20},{28,24},{32,28},{36,32}... | collective-permute-start | bytes 1572872 | tf_op jit(solution)/shard_map/ppermute | solution.py:27
  13.1 4.1 %collective-permute-done = f32[4,16,2048]{2,1,0:T(8,128)} collective-permute-done((f32[4,16,2048]{2,1,0:T(8,128)}, f32[4,16,2048]{2,1,0:T(8,128)}, u32[]{:S(2)}, u32[]{:S(2)}) %collective-permute-start) | collective-permute-done | bytes 524320 | tf_op jit(solution)/shard_map/ppermute | solution.py:24
  17.2 4.4 %collective-permute-done.1 = f32[4,16,2048]{2,1,0:T(8,128)} collective-permute-done((f32[4,16,2048]{2,1,0:T(8,128)}, f32[4,16,2048]{2,1,0:T(8,128)}, u32[]{:S(2)}, u32[]{:S(2)}) %collective-permute-start.1) | collective-permute-done | bytes 524320 | tf_op jit(solution)/shard_map/ppermute | solution.py:27
  21.6 1.7 %pad_maximum_fusion = f32[4,160,2048]{2,1,0:T(8,128)S(1)} fusion(f32[4,16,2048]{2,1,0:T(8,128)} %collective-permute-done.1, f32[1,128,2048]{2,1,0:T(8,128)} %copy-done.1, f32[1,128,2048]{2,1,0:T(8,128)S(1)} %get-tuple-element.28, f32[1,128,2048]{2,1,0:T(8,128)S(1)} %get-tuple-element.25, f32[1,128,2048]{2,1,0:T(8,128)S(1)} %get-tuple-element.24, ...), kind=kLoop, calls=%fused_computation.4 | loop fusion | flops 6553600 | bytes 10485760 | tf_op jit(solution)/shard_map/concatenate | solution.py:28
  23.4 0.0 copy-start
  23.4 2.4 %copy-done = f32[4,160,2048]{2,1,0:T(8,128)} copy-done((f32[4,160,2048]{2,1,0:T(8,128)}, f32[4,160,2048]{2,1,0:T(8,128)S(1)}, u32[]{:S(2)}) %copy-start) | copy-done | bytes 5242904
  25.7 0.2 fusion.42
  25.9 3.2 %collective-permute-start.2 = (f32[4,160,4]{2,1,0:T(8,128)S(1)}, f32[4,160,4]{2,1,0:T(8,128)S(1)}, u32[]{:S(2)}, u32[]{:S(2)}) collective-permute-start(f32[4,160,4]{2,1,0:T(8,128)S(1)} %get-tuple-element.23), channel_id=1, source_target_pairs={{0,1},{1,2},{2,3},{4,5},{5,6},{6,7},{8,9},{9,10},{10,11},{12,13},{... | collective-permute-start | bytes 30728 | tf_op jit(solution)/shard_map/ppermute | solution.py:24
  29.1 1.3 %collective-permute-start.3 = (f32[4,160,4]{2,1,0:T(8,128)S(1)}, f32[4,160,4]{2,1,0:T(8,128)S(1)}, u32[]{:S(2)}, u32[]{:S(2)}) collective-permute-start(f32[4,160,4]{2,1,0:T(8,128)S(1)} %get-tuple-element.22), channel_id=1, source_target_pairs={{1,0},{2,1},{3,2},{5,4},{6,5},{7,6},{9,8},{10,9},{11,10},{13,12},{... | collective-permute-start | bytes 30728 | tf_op jit(solution)/shard_map/ppermute | solution.py:27
  30.5 2.7 %collective-permute-done.2 = f32[4,160,4]{2,1,0:T(8,128)S(1)} collective-permute-done((f32[4,160,4]{2,1,0:T(8,128)S(1)}, f32[4,160,4]{2,1,0:T(8,128)S(1)}, u32[]{:S(2)}, u32[]{:S(2)}) %collective-permute-start.2) | collective-permute-done | bytes 10272 | tf_op jit(solution)/shard_map/ppermute | solution.py:24
  33.1 3.8 %collective-permute-done.3 = f32[4,160,4]{2,1,0:T(8,128)S(1)} collective-permute-done((f32[4,160,4]{2,1,0:T(8,128)S(1)}, f32[4,160,4]{2,1,0:T(8,128)S(1)}, u32[]{:S(2)}, u32[]{:S(2)}) %collective-permute-start.3) | collective-permute-done | bytes 10272 | tf_op jit(solution)/shard_map/ppermute | solution.py:27
  37.0 7.2 %concatenate.10 = f32[4,160,2056]{2,1,0:T(8,128)} concatenate(f32[4,160,4]{2,1,0:T(8,128)S(1)} %collective-permute-done.2, f32[4,160,2048]{2,1,0:T(8,128)} %copy-done, f32[4,160,4]{2,1,0:T(8,128)S(1)} %collective-permute-done.3), dimensions={2} | concatenate | bytes 10526720 | tf_op jit(solution)/shard_map/concatenate | solution.py:28
  44.1 4.8 %slice_add_fusion.2 = f32[4,159,2056]{2,1,0:T(8,128)S(1)} fusion(f32[4,160,2056]{2,1,0:T(8,128)} %concatenate.10), kind=kLoop, calls=%fused_computation.2 | loop fusion | flops 1307616 | bytes 15691392 | tf_op jit(solution)/shard_map/add | solution.py:40
  48.9 0.5 slice_add_fusion.1
  49.5 0.5 slice_add_fusion
  50.0 0.4 slice_add_fusion.3
  50.4 0.3 slice_add_fusion.7
  50.7 1.3 %slice_add_fusion.6 = f32[4,129,2055]{2,1,0:T(8,128)S(1)} fusion(f32[4,129,2056]{2,1,0:T(8,128)S(1)} %slice_add_fusion.7), kind=kLoop, calls=%fused_computation.7 | loop fusion | flops 1060380 | bytes 12724560 | tf_op jit(solution)/shard_map/add | solution.py:40
  52.0 1.3 %slice_add_fusion.5 = f32[4,129,2053]{2,1,0:T(8,128)S(1)} fusion(f32[4,129,2055]{2,1,0:T(8,128)S(1)} %slice_add_fusion.6), kind=kLoop, calls=%fused_computation.6 | loop fusion | flops 1059348 | bytes 12712176 | tf_op jit(solution)/shard_map/add | solution.py:40
  53.3 1.3 %slice_add_fusion.4 = f32[4,129,2049]{2,1,0:T(8,128)S(1)} fusion(f32[4,129,2053]{2,1,0:T(8,128)S(1)} %slice_add_fusion.5), kind=kLoop, calls=%fused_computation.5 | loop fusion | flops 1057284 | bytes 12687408 | tf_op jit(solution)/shard_map/add | solution.py:40
  54.6 0.0 copy-start.2
  54.7 0.0 copy-start.3
  54.7 1.8 %fusion.14 = (f32[128,2048]{1,0:T(8,128)}, f32[1,128,2048]{2,1,0:T(8,128)S(1)}, f32[1,128,2048]{2,1,0:T(8,128)S(1)}) fusion(f32[4,129,2049]{2,1,0:T(8,128)S(1)} %slice_add_fusion.4), kind=kLoop, calls=%fused_computation.34 | loop fusion | flops 2097152 | bytes 7340032 | tf_op jit(solution)/shard_map/sqrt | solution.py:91
  56.4 0.0 copy-done.2
  56.4 0.7 multiply_reduce_fusion
  57.2 0.0 copy-done.3
  57.2 0.2 fusion.20
  57.4 9.5 %psum.28 = f32[16,12]{1,0:T(8,128)S(1)} all-reduce(f32[16,12]{1,0:T(8,128)S(1)} %fusion.20), channel_id=1, replica_groups=mesh['rows_0'=4,'rows_1'=8,'rows_2'=2,'cols'=4] {'rows_0'}, use_global_device_ids=true, to_apply=%region_7.0 | all-reduce | flops 192 | bytes 1536 | tf_op jit(solution)/shard_map/psum | solution.py:33
  66.9 17.2 %psum.29 = f32[16,12]{1,0:T(8,128)S(1)} all-reduce(f32[16,12]{1,0:T(8,128)S(1)} %psum.28), channel_id=1, replica_groups=mesh['rows_0'=4,'rows_1'=8,'rows_2'=2,'cols'=4] {'rows_1'}, use_global_device_ids=true, to_apply=%region_8.0 | all-reduce | flops 192 | bytes 1536 | tf_op jit(solution)/shard_map/psum | solution.py:33
  84.1 8.3 %psum.30 = f32[16,12]{1,0:T(8,128)S(1)} all-reduce(f32[16,12]{1,0:T(8,128)S(1)} %psum.29), channel_id=1, replica_groups=mesh['rows_0'=4,'rows_1'=8,'rows_2'=2,'cols'=4] {'rows_2'}, use_global_device_ids=true, to_apply=%region_9.0 | all-reduce | flops 192 | bytes 1536 | tf_op jit(solution)/shard_map/psum | solution.py:33
  92.5 7.4 %psum.31 = f32[16,12]{1,0:T(8,128)S(1)} all-reduce(f32[16,12]{1,0:T(8,128)S(1)} %psum.30), channel_id=1, replica_groups=mesh['rows_0'=4,'rows_1'=8,'rows_2'=2,'cols'=4] {'cols'}, use_global_device_ids=true, to_apply=%region_10.0 | all-reduce | flops 192 | bytes 1536 | tf_op jit(solution)/shard_map/psum | solution.py:33
  99.8 0.2 fusion.41
  100.0 0.1 fusion.29
  100.1 0.1 fusion.31
  100.3 0.2 fusion.40
  100.4 0.1 subtract_divide_fusion.1
  100.5 0.2 fusion.18
  100.8 0.3 bitcast_multiply_fusion.9
  101.0 0.2 convolution_bitcast_fusion.1
  101.3 0.8 fusion.5
  102.1 1.5 %pad_maximum_fusion.1 = f32[2,128,2048]{2,1,0:T(8,128)} fusion(f32[1,128,2048]{2,1,0:T(8,128)S(1)} %get-tuple-element.31, f32[1,128,2048]{2,1,0:T(8,128)S(1)} %get-tuple-element.30), kind=kLoop, calls=%fused_computation.9 | loop fusion | flops 524288 | bytes 4194304 | tf_op jit(solution)/shard_map/stack | solution.py:191
  (5 shorter events, 0.1 us)
Async XLA Ops:
  3.9 1.0 copy-start.1
  5.9 11.3 %collective-permute-start = (f32[4,16,2048]{2,1,0:T(8,128)}, f32[4,16,2048]{2,1,0:T(8,128)}, u32[]{:S(2)}, u32[]{:S(2)}) collective-permute-start(f32[4,16,2048]{2,1,0:T(8,128)} %get-tuple-element.26), channel_id=1, source_target_pairs={{0,4},{4,8},{8,12},{12,16},{16,20},{20,24},{24,28},{28,32},{32,36}... | collective-permute-start | bytes 1572872 | tf_op jit(solution)/shard_map/ppermute | solution.py:24
  10.8 10.8 %collective-permute-start.1 = (f32[4,16,2048]{2,1,0:T(8,128)}, f32[4,16,2048]{2,1,0:T(8,128)}, u32[]{:S(2)}, u32[]{:S(2)}) collective-permute-start(f32[4,16,2048]{2,1,0:T(8,128)} %get-tuple-element.27), channel_id=1, source_target_pairs={{4,0},{8,4},{12,8},{16,12},{20,16},{24,20},{28,24},{32,28},{36,32}... | collective-permute-start | bytes 1572872 | tf_op jit(solution)/shard_map/ppermute | solution.py:27
  23.4 2.4 %copy-start = (f32[4,160,2048]{2,1,0:T(8,128)}, f32[4,160,2048]{2,1,0:T(8,128)S(1)}, u32[]{:S(2)}) copy-start(f32[4,160,2048]{2,1,0:T(8,128)S(1)} %pad_maximum_fusion) | copy-start | bytes 15728644
  25.9 7.2 %collective-permute-start.2 = (f32[4,160,4]{2,1,0:T(8,128)S(1)}, f32[4,160,4]{2,1,0:T(8,128)S(1)}, u32[]{:S(2)}, u32[]{:S(2)}) collective-permute-start(f32[4,160,4]{2,1,0:T(8,128)S(1)} %get-tuple-element.23), channel_id=1, source_target_pairs={{0,1},{1,2},{2,3},{4,5},{5,6},{6,7},{8,9},{9,10},{10,11},{12,13},{... | collective-permute-start | bytes 30728 | tf_op jit(solution)/shard_map/ppermute | solution.py:24
  29.1 7.8 %collective-permute-start.3 = (f32[4,160,4]{2,1,0:T(8,128)S(1)}, f32[4,160,4]{2,1,0:T(8,128)S(1)}, u32[]{:S(2)}, u32[]{:S(2)}) collective-permute-start(f32[4,160,4]{2,1,0:T(8,128)S(1)} %get-tuple-element.22), channel_id=1, source_target_pairs={{1,0},{2,1},{3,2},{5,4},{6,5},{7,6},{9,8},{10,9},{11,10},{13,12},{... | collective-permute-start | bytes 30728 | tf_op jit(solution)/shard_map/ppermute | solution.py:27
  54.6 1.8 %copy-start.2 = (s32[128,2048]{1,0:T(8,128)S(1)}, s32[128,2048]{1,0:T(8,128)}, u32[]{:S(2)}) copy-start(s32[128,2048]{1,0:T(8,128)} %param.6) | copy-start | bytes 3145732
  54.7 2.6 %copy-start.3 = (s32[128]{0:T(128)S(1)}, s32[128]{0:T(128)}, u32[]{:S(2)}) copy-start(s32[128]{0:T(128)} %param.7) | copy-start | bytes 1540
where the time goes:
time: 104 us
  blocking collectives  42.4 us (41%)
  other arithmetic  22 us (21%)
  waiting for transfers between devices  15 us (14%)
  starting transfers between devices  11.7 us (11%)
  local copies, waits for them, and re-layouts  10.7 us (10%)
    psum x4, blocking collectives, by_axis(): return functools.reduce(lax.psum, axes, shard)  42.4 us
    add x8, other arithmetic, window_sum(): lax.slice_in_dim(planes, 0, extent - offset, axis=along_dim)  10.5 us
    ppermute x2, waiting for transfers between devices, extended(): lax.ppermute(lax.slice_in_dim(block, 0, width, axis=dim), axis, backward)  8.23 us
    ppermute x2, starting transfers between devices, extended(): lax.ppermute(lax.slice_in_dim(block, block.shape[dim] - width, None, axis...  8.13 us
    concatenate x1, local copies, waits for them, and re-layouts, extended(): block = jnp.concatenate([low, block, high], axis=dim)  7.18 us
    ppermute x2, waiting for transfers between devices, extended(): lax.ppermute(lax.slice_in_dim(block, block.shape[dim] - width, None, axis...  6.78 us
    ppermute x2, starting transfers between devices, extended(): lax.ppermute(lax.slice_in_dim(block, 0, width, axis=dim), axis, backward)  3.57 us
    unnamed x8, local copies, waits for them, and re-layouts  3.33 us
  transfers between devices with their start and end apart: 4, of which 4 were waited for; matrix products, arithmetic and copies ran while one was open for 0% of the time, Pallas kernels for 0%

commit v1 on v0

v1 whole, which is shorter than its diff:
```python
import functools

import jax
import jax.numpy as jnp
from jax import lax
from jax.experimental import pallas as pl
from jax.experimental.pallas import tpu as pltpu
from jax.sharding import PartitionSpec as P

WIN_R = 32
WIN_C = 8
SWEEP_TALLY = 16
HALO = WIN_R // 2
SIDE = WIN_C // 2
LANES = 128
REACH = 8
MESH = pl.DeviceIdType.MESH
F32 = jnp.float32
BF16 = jnp.bfloat16
EXACT = lax.Precision.HIGHEST


def split_pair(x):
    high = x.astype(BF16)
    return high, (x - high.astype(F32)).astype(BF16)


def lane_of(shape):
    return lax.broadcasted_iota(jnp.int32, shape, 1)


def row_of(shape):
    return lax.broadcasted_iota(jnp.int32, shape, 0)


def gamma_kernel(
    count_rows, count_cols,
    lead, trail, flags, sweep,
    gamma, coefs,
    first, second, weight, planes, boxed, up_out, down_out, above, below, left_out, right_out, left_in, right_in,
    side_boxed, side_planes, band, side_band, tri, halo_planes, sums, membership, table, from_cols, table_rows, from_rows,
    load_sem, row_send, row_recv, col_send, col_recv, ysend, yrecv, rsend, rrecv, token,
):
    rows, cols = weight.shape
    blocks = cols // LANES
    my_row = lax.axis_index("rows")
    my_col = lax.axis_index("cols")

    def at(d_row, d_col):
        return {
            "rows": lax.rem(my_row + d_row + count_rows, count_rows),
            "cols": lax.rem(my_col + d_col + count_cols, count_cols),
        }

    def signal(sem, where):
        pl.semaphore_signal(sem, inc=1, device_id=where, device_id_type=MESH)

    barrier = pltpu.get_barrier_semaphore()
    near = [(a, b) for a in (-1, 0, 1) for b in (-1, 0, 1) if (a, b) != (0, 0)] + [(0, 2)]
    for offset in near:
        signal(barrier, at(*offset))

    loads = []

    def load(low, high, left, right):
        started = []
        window = (pl.ds(low, high - low), pl.ds(left, right - left))
        for source, target in ((lead, first), (trail, second)):
            started.append((source.at[(slice(None),) + window], target.at[(slice(None),) + window]))
        started.append((flags.at[window], weight.at[window]))
        copies = []
        for source, target in started:
            copy = pltpu.make_async_copy(source, target, load_sem.at[len(loads)])
            copy.start()
            loads.append(copy)
            copies.append(copy)
        return copies

    def arrive(copies):
        for copy in copies:
            copy.wait()

    inner = rows - HALO
    edge_loads = load(0, HALO, 0, cols) + load(inner, rows, 0, cols)
    side_loads = load(HALO, inner, 0, LANES) + load(HALO, inner, cols - LANES, cols)
    step = (inner - HALO) // 3
    main_loads = [load(HALO + i * step, HALO + (i + 1) * step, LANES, cols - LANES) for i in range(3)]

    box_row = row_of((rows, 2 * rows))
    box_col = lax.rem(lane_of((rows, 2 * rows)), rows) - box_row
    band[...] = jnp.where((box_col >= -HALO) & (box_col < HALO), 1.0, 0.0).astype(BF16)
    tall = rows + 2 * HALO
    side_row = row_of((rows, 2 * tall))
    side_col = lax.rem(lane_of((rows, 2 * tall)), tall) - side_row
    side_line = side_col + side_row
    side_exists = ((side_line >= HALO) | (my_row > 0)) & ((side_line < rows + HALO) | (my_row < count_rows - 1))
    side_band[...] = jnp.where((side_col >= 0) & (side_col < WIN_R) & side_exists, 1.0, 0.0).astype(BF16)
    tri_row = row_of((2 * HALO, 4 * HALO))
    tri_lane = lane_of((2 * HALO, 4 * HALO))
    tri_col = lax.rem(tri_lane, HALO)
    has_above = jnp.where(my_row > 0, 1.0, 0.0)
    has_below = jnp.where(my_row < count_rows - 1, 1.0, 0.0)
    tri_above = jnp.where((tri_row < HALO) & (tri_lane < 2 * HALO) & (tri_col >= tri_row), has_above, 0.0)
    tri_below = jnp.where((tri_row >= HALO) & (tri_lane >= 2 * HALO) & (tri_col < tri_row - HALO), has_below, 0.0)
    tri[...] = (tri_above + tri_below).astype(BF16)
    along = ((my_row * rows + lane_of((LANES, rows))).astype(F32) + 0.5) * (2.0 / (rows * count_rows)) - 1.0
    burst = row_of((LANES, rows))
    power = burst // SWEEP_TALLY
    chosen = jnp.where((burst - power * SWEEP_TALLY == sweep[...]) & (power < 3), 1.0, 0.0)
    membership[1] = chosen * jnp.where(power == 0, 1.0, jnp.where(power == 1, along, along * along))
    membership[0] = jnp.transpose(jnp.where(burst == sweep[...], 1.0, 0.0))

    lane = lane_of((8, LANES))
    lane16 = lane_of((HALO, LANES))

    def products(row, block):
        here = (pl.ds(row, HALO), pl.ds(block * LANES, LANES))
        w = weight[here].astype(F32)
        real_a, imag_a = first[(0,) + here] * w, first[(1,) + here] * w
        real_b, imag_b = second[(0,) + here] * w, second[(1,) + here] * w
        return (
            real_a * real_b + imag_a * imag_b,
            imag_a * real_b - real_a * imag_b,
            real_a * real_a + imag_a * imag_a,
            real_b * real_b + imag_b * imag_b,
        )

    def fill(row, sends=None):
        for block in range(blocks):
            here = pl.ds(block * LANES, LANES)
            for p, x in enumerate(products(row, block)):
                if sends is not None:
                    sends[p, :, here] = x
                high, low = split_pair(x)
                planes[p, pl.ds(row, HALO), here] = high
                planes[p, pl.ds(rows + row, HALO), here] = low

    arrive(edge_loads)
    fill(0, up_out)
    fill(inner, down_out)
    arrive(side_loads)

    @pl.loop(0, rows // HALO)
    def _(group):
        row = pl.multiple_of(group * HALO, HALO)
        packed_left = jnp.zeros((HALO, LANES), F32)
        packed_right = jnp.zeros((HALO, LANES), F32)
        for p, x in enumerate(products(row, 0)):
            x = jnp.where(lane16 < SIDE, x, 0.0)
            packed_left += x if p == 0 else pltpu.roll(x, SIDE * p, 1)
        for p, x in enumerate(products(row, blocks - 1)):
            packed_right += pltpu.roll(jnp.where(lane16 >= LANES - SIDE, x, 0.0), SIDE * (p + 1), 1)
        left_out[pl.ds(row, HALO), :] = packed_left
        right_out[pl.ds(row, HALO), :] = packed_right

    pl.semaphore_wait(barrier, len(near))

    def send(source, target, send_sem, recv_sem, where):
        copy = pltpu.make_async_remote_copy(
            src_ref=source, dst_ref=target, send_sem=send_sem, recv_sem=recv_sem, device_id=where, device_id_type=MESH
        )
        copy.start()
        return copy

    row_copies = [
        send(up_out, below, row_send.at[0], row_recv.at[0], at(-1, 0)),
        send(down_out, above, row_send.at[1], row_recv.at[1], at(1, 0)),
    ]
    col_copies = []
    for source, target, d_col in ((left_out, right_in, -1), (right_out, left_in, 1)):
        for low, size, to, d_row in ((0, rows, HALO, 0), (0, HALO, rows + HALO, -1), (inner, HALO, 0, 1)):
            i = len(col_copies)
            col_copies.append(
                send(
                    source.at[pl.ds(low, size), :], target.at[pl.ds(to, size), :],
                    col_send.at[i], col_recv.at[i], at(d_row, d_col),
                )
            )
    for d in (-1, 1):
        signal(token.at[0], at(d, 0))

    for i, copies in enumerate(main_loads):
        arrive(copies)

        @pl.loop(HALO + i * step, HALO + (i + 1) * step, step=HALO)
        def _(row):
            fill(pl.multiple_of(row, HALO))

    pl.semaphore_wait(token.at[0], 2)
    for d in (-2, 2):
        signal(token.at[1], at(d, 0))

    wide = 2 * LANES
    for p in range(4):
        @pl.loop(0, cols // wide)
        def _(n):
            here = pl.ds(pl.multiple_of(n * wide, wide), wide)
            boxed[p, :, here] = jnp.dot(band[...], planes[p, :, here], preferred_element_type=F32)

    for copy in col_copies:
        copy.wait()
    for i, (arrived, exists) in enumerate(((left_in, my_col > 0), (right_in, my_col < count_cols - 1))):
        high, low = split_pair(arrived[...] * jnp.where(exists, 1.0, 0.0))
        side_planes[pl.ds(0, tall), pl.ds(i * LANES, LANES)] = high
        side_planes[pl.ds(tall, tall), pl.ds(i * LANES, LANES)] = low
    side_boxed[...] = jnp.dot(side_band[...], side_planes[...], preferred_element_type=F32)

    across_first = ((my_col * cols + lane).astype(F32) + 0.5) * (2.0 / (cols * count_cols)) - 1.0

    def finish(group):
        here = pl.ds(pl.multiple_of(group * 8, 8), 8)
        packed = side_boxed[here, pl.ds(0, LANES)], side_boxed[here, pl.ds(LANES, LANES)]

        def block(p, j):
            if j == 0:
                return pltpu.roll(packed[0], LANES - SIDE * (p + 1), 1)
            if j == blocks + 1:
                return packed[1] if p == 0 else pltpu.roll(packed[1], LANES - SIDE * p, 1)
            return boxed[p, here, pl.ds((j - 1) * LANES, LANES)]

        one, one_turned, two, two_turned, four_turned = ({} for _ in range(5))
        raw, raw_turned = {}, {}
        totals = [jnp.zeros((8, LANES), F32) for _ in range(7)]
        for j in range(blocks + 2):
            for p in range(4):
                raw[p, j] = block(p, j)
                raw_turned[p, j] = pltpu.roll(raw[p, j], LANES - 1, 1)
                ready = [j - 1] if j else []
                if j == blocks + 1:
                    ready.append(j)
                for k in ready:
                    follow = raw_turned[p, min(k + 1, j)]
                    one[p, k] = raw[p, k] + jnp.where(lane < LANES - 1, raw_turned[p, k], follow)
                    one_turned[p, k] = pltpu.roll(one[p, k], LANES - 2, 1)
                    if k:
                        i = k - 1
                        two[p, i] = one[p, i] + jnp.where(lane < LANES - 2, one_turned[p, i], one_turned[p, k])
                        two_turned[p, i] = pltpu.roll(two[p, i], SIDE, 1)
            done = [j - 2] if j >= 3 else []
            if j == blocks + 1:
                done.append(j - 1)
            for i in done:
                real, imag, power_a, power_b = (
                    two[p, i] + jnp.where(lane >= SIDE, two_turned[p, i], two_turned[p, i - 1]) for p in range(4)
                )
                scale = lax.rsqrt((power_a + 1.0) * (power_b + 1.0))
                real, imag = real * scale, imag * scale
                there = pl.ds((i - 1) * LANES, LANES)
                gamma[0, here, there] = real
                gamma[1, here, there] = imag
                w = weight[here, there].astype(F32)
                across = across_first + (i - 1) * (LANES * 2.0 / (cols * count_cols))
                wu = w * across
                terms = (w, wu, wu * across, w * real, w * imag, wu * real, wu * imag)
                totals = [total + term for total, term in zip(totals, terms)]
        for q, total in enumerate(totals):
            sums[here, pl.ds(q * LANES, LANES)] = total

    @pl.loop(HALO // 8, inner // 8)
    def _(group):
        finish(group)

    pl.semaphore_wait(token.at[1], 2)
    for d in (-4, 4):
        signal(token.at[2], at(d, 0))

    for copy in row_copies:
        copy.wait()
    for p in range(4):
        for i, arrived in enumerate((above, below)):
            high, low = split_pair(arrived[p])
            halo_planes[p, pl.ds(2 * i * HALO, HALO), :] = high
            halo_planes[p, pl.ds((2 * i + 1) * HALO, HALO), :] = low

        @pl.loop(0, cols // wide)
        def _(n):
            there = pl.ds(pl.multiple_of(n * wide, wide), wide)
            extra = jnp.dot(tri[...], halo_planes[p, :, there], preferred_element_type=F32)
            boxed[p, pl.ds(0, HALO), there] += extra[:HALO]
            boxed[p, pl.ds(inner, HALO), there] += extra[HALO:]

    @pl.loop(0, 2 * HALO // 8)
    def _(i):
        finish(jnp.where(i < HALO // 8, i, i + (inner - HALO) // 8))

    by_burst = jnp.dot(membership[1], sums[...], preferred_element_type=F32, precision=EXACT)
    kind = lane_of((8, 7 * LANES)) // LANES
    pick = jnp.where(kind == row_of((8, 7 * LANES)), 1.0, 0.0)
    table[...] = lax.dot_general(
        pick, by_burst, (((1,), (1,)), ((), ())), preferred_element_type=F32, precision=EXACT
    )

    copies = [
        send(table, from_cols.at[k - 1], ysend.at[k - 1], yrecv.at[k - 1], at(0, k)) for k in range(1, 4)
    ]
    pl.semaphore_wait(token.at[2], 2)
    for copy in copies:
        copy.wait()
    table_rows[...] = (table[...] + from_cols[0]) + (from_cols[1] + from_cols[2])
    distances = [d for k in range(1, REACH + 1) for d in (-k, k)]
    copies = [
        send(table_rows, from_rows.at[i], rsend.at[i], rrecv.at[i], at(d, 0)) for i, d in enumerate(distances)
    ]
    for copy in copies:
        copy.wait()
    total = table_rows[...]
    for i in range(len(distances)):
        total = total + from_rows[i]

    once = pltpu.roll(total, LANES - SWEEP_TALLY, 1)
    twice = pltpu.roll(total, LANES - 2 * SWEEP_TALLY, 1)
    count, sum_u, sum_uu, h0_re, h0_im, hu_re, hu_im = (total[q:q + 1] for q in range(7))
    sum_v, sum_uv, hv_re, hv_im = (once[q:q + 1] for q in (0, 1, 3, 4))
    sum_vv = twice[0:1]
    floored = jnp.maximum(count, 1.0)
    mean_u = sum_u / floored
    mean_v = sum_v / floored
    guu = sum_uu - 2.0 * mean_u * sum_u + mean_u * mean_u * count
    guv = sum_uv - mean_u * sum_v - mean_v * sum_u + mean_u * mean_v * count
    gvv = sum_vv - 2.0 * mean_v * sum_v + mean_v * mean_v * count
    ridge = 0.001 * count + 1.0
    diag_u = guu + ridge
    diag_v = gvv + ridge
    inverse = 1.0 / (diag_u * diag_v - guv * guv)
    base = 1.0 / (count + ridge)
    out = []
    slopes_u, slopes_v = [], []
    for h0, hu, hv in ((h0_re, hu_re, hv_re), (h0_im, hu_im, hv_im)):
        hu = hu - mean_u * h0
        hv = hv - mean_v * h0
        out.append(h0 * base)
        slopes_u.append((diag_v * hu - guv * hv) * inverse)
        slopes_v.append((diag_u * hv - guv * hu) * inverse)
    entries = out + slopes_u + slopes_v + [mean_u, mean_v]
    stacked = jnp.zeros((LANES, LANES), F32)
    place = row_of((LANES, LANES))
    for i, entry in enumerate(entries):
        stacked = jnp.where(place == i, entry, stacked)
    stacked = jnp.where(lane_of((LANES, LANES)) < SWEEP_TALLY, stacked, 0.0)
    coefs[...] = lax.dot_general(
        membership[0], stacked, (((1,), (1,)), ((), ())), preferred_element_type=F32, precision=EXACT
    )


def ramp_kernel(count_rows, count_cols, gamma, coefs, deramped, coherence, out, size, sem):
    _, rows, cols = gamma.shape
    my_row = lax.axis_index("rows")
    my_col = lax.axis_index("cols")
    lane = lane_of((8, LANES))
    across_first = ((my_col * cols + lane).astype(F32) + 0.5) * (2.0 / (cols * count_cols)) - 1.0
    chunk = 32
    copies = []
    for low in range(0, rows, chunk):
        @pl.loop(low // 8, (low + chunk) // 8)
        def _(group):
            start = pl.multiple_of(group * 8, 8)
            here = pl.ds(start, 8)
            line = coefs[here, :]
            along = ((my_row * rows + start + row_of((8, LANES))).astype(F32) + 0.5) * (
                2.0 / (rows * count_rows)
            ) - 1.0
            wide = [jnp.broadcast_to(line[:, q:q + 1], (8, LANES)) for q in range(8)]
            along = along - wide[7]
            base_re = wide[0] + wide[4] * along
            base_im = wide[1] + wide[5] * along
            centred = across_first - wide[6]
            for j in range(cols // LANES):
                there = pl.ds(j * LANES, LANES)
                du = centred + j * (LANES * 2.0 / (cols * count_cols))
                model_re = base_re + wide[2] * du
                model_im = base_im + wide[3] * du
                real, imag = gamma[0, here, there], gamma[1, here, there]
                out[0, here, there] = real * model_re + imag * model_im
                out[1, here, there] = imag * model_re - real * model_im
                size[here, there] = jnp.sqrt(real * real + imag * imag)

        here = pl.ds(low, chunk)
        for source, target in ((out.at[:, here, :], deramped.at[:, here, :]), (size.at[here, :], coherence.at[here, :])):
            copy = pltpu.make_async_copy(source, target, sem.at[len(copies)])
            copy.start()
            copies.append(copy)
    for copy in copies:
        copy.wait()


def on_device(count_rows, count_cols, lead, trail, flags, sweep):
    rows, cols = flags.shape
    tall = rows + 2 * HALO
    vmem = pl.BlockSpec(memory_space=pltpu.VMEM)
    hbm = pl.BlockSpec(memory_space=pl.ANY)
    dma = pltpu.SemaphoreType.DMA
    V = pltpu.VMEM
    gamma, coefs = pl.pallas_call(
        functools.partial(gamma_kernel, count_rows, count_cols),
        out_shape=(V((2, rows, cols), F32), V((rows, LANES), F32)),
        in_specs=[hbm, hbm, hbm, vmem],
        out_specs=(vmem, vmem),
        scratch_shapes=[
            V((2, rows, cols), F32), V((2, rows, cols), F32), V((rows, cols), jnp.int32),
            V((4, 2 * rows, cols), BF16), V((4, rows, cols), F32),
            V((4, HALO, cols), F32), V((4, HALO, cols), F32), V((4, HALO, cols), F32), V((4, HALO, cols), F32),
            V((rows, LANES), F32), V((rows, LANES), F32), V((tall, LANES), F32), V((tall, LANES), F32),
            V((rows, 2 * LANES), F32), V((2 * tall, 2 * LANES), BF16),
            V((rows, 2 * rows), BF16), V((rows, 2 * tall), BF16), V((2 * HALO, 4 * HALO), BF16),
            V((4, 4 * HALO, cols), BF16), V((rows, 7 * LANES), F32), V((2, LANES, rows), F32),
            V((8, LANES), F32), V((3, 8, LANES), F32), V((8, LANES), F32), V((2 * REACH, 8, LANES), F32),
            dma((21,)), dma((2,)), dma((2,)), dma((6,)), dma((6,)), dma((3,)), dma((3,)),
            dma((2 * REACH,)), dma((2 * REACH,)), pltpu.SemaphoreType.REGULAR((3,)),
        ],
        compiler_params=pltpu.CompilerParams(
            collective_id=0, has_side_effects=True, vmem_limit_bytes=40 * 1024 * 1024
        ),
        name="coherence",
    )(lead, trail, flags, sweep.reshape(1, rows))
    return pl.pallas_call(
        functools.partial(ramp_kernel, count_rows, count_cols),
        out_shape=(
            jax.ShapeDtypeStruct((2, rows, cols), F32),
            jax.ShapeDtypeStruct((rows, cols), F32),
        ),
        in_specs=[vmem, vmem],
        out_specs=(hbm, hbm),
        scratch_shapes=[V((2, rows, cols), F32), V((rows, cols), F32), dma((8,))],
        compiler_params=pltpu.CompilerParams(vmem_limit_bytes=16 * 1024 * 1024),
        name="ramp",
    )(gamma, coefs)


def solution(mesh):
    in_specs = (P(None, "rows", "cols"), P(None, "rows", "cols"), P("rows", "cols"), P("rows"))
    out_specs = (P(None, "rows", "cols"), P("rows", "cols"))
    body = functools.partial(on_device, mesh.shape["rows"], mesh.shape["cols"])
    return jax.shard_map(body, mesh=mesh, in_specs=in_specs, out_specs=out_specs, check_vma=False)
```

time: 104 us -> 49.8 us (0.48)
  Pallas kernels: 0 us -> 43.9 us
  blocking collectives: 42.4 us -> 0 us
  other arithmetic: 22 us -> 0 us
  waiting for transfers between devices: 15 us -> 0 us
  starting transfers between devices: 11.7 us -> 0 us
  local copies, waits for them, and re-layouts: 10.7 us -> 5.05 us
    pallas_call x0 -> x2, Pallas kernels: none -> 43.9 us  [the longest x1 41.3 us: on_device(): pl.pallas_call(functools.partial(gamma_kernel, count_rows, count_cols), o...]
    psum x4 -> x0, blocking collectives: 42.4 us -> none  [by_axis(): return functools.reduce(lax.psum, axes, shard)]
    ppermute x4 -> x0, waiting for transfers between devices: 15 us -> none  [the longest x2 8.23 us: extended(): lax.ppermute(lax.slice_in_dim(block, 0, width, axis=dim), axis, backward)]
    add x12 -> x0, other arithmetic: 11.7 us -> none  [the longest x8 10.5 us: window_sum(): lax.slice_in_dim(planes, 0, extent - offset, axis=along_dim)]
    ppermute x4 -> x0, starting transfers between devices: 11.7 us -> none  [the longest x2 8.13 us: extended(): lax.ppermute(lax.slice_in_dim(block, block.shape[dim] - width, None, axis...]
    concatenate x1 -> x0, local copies, waits for them, and re-layouts: 7.18 us -> none  [extended(): block = jnp.concatenate([low, block, high], axis=dim)]
    another operation x2 -> x0, other arithmetic: 4.69 us -> none  [the longest x1 3.23 us: form_products(): jnp.stack([real_a * real_b + imag_a * imag_b, imag_a * real_b - real_a *...]
    sqrt x1 -> x0, other arithmetic: 1.77 us -> none  [on_device(): coherence = jnp.sqrt(coh_real * coh_real + coh_imag * coh_imag)]
  transfers between devices with their start and end apart: 4 -> 0, of which waited for: 4 -> 0; matrix products, arithmetic and copies ran while one was open for 0% -> 0% of each run, Pallas kernels for 0% -> 0%
where the time goes in v1:
time: 49.8 us; the launch traced here: 49.6 us
  Pallas kernels  43.9 us (88%)
  local copies, waits for them, and re-layouts  5.05 us (10%)
  between operations  0.65 us (1%)
    pallas_call x1, Pallas kernels, on_device(): pl.pallas_call(functools.partial(gamma_kernel, count_rows, count_cols), o...  41.3 us
    unnamed x8, local copies, waits for them, and re-layouts  5.05 us
    pallas_call x1, Pallas kernels, on_device(): pl.pallas_call(functools.partial(ramp_kernel, count_rows, count_cols), ou...  2.61 us

profile of v1, /device:TPU:1, one launch (start us, length us, event | category | flops | bytes accessed | tf_op | source)
XLA Modules:
  0.0 49.6 jit_solution(10503681340476776083)
XLA Ops:
  0.6 0.0 copy-start
  0.6 1.6 %copy-done = f32[2,128,2048]{2,1,0:T(8,128)S(1)} copy-done((f32[2,128,2048]{2,1,0:T(8,128)S(1)}, f32[2,128,2048]{2,1,0:T(8,128)}, u32[]{:S(2)}) %copy-start) | copy-done | bytes 2097176
  2.2 0.0 copy-start.1
  2.2 1.6 %copy-done.1 = f32[2,128,2048]{2,1,0:T(8,128)S(1)} copy-done((f32[2,128,2048]{2,1,0:T(8,128)S(1)}, f32[2,128,2048]{2,1,0:T(8,128)}, u32[]{:S(2)}) %copy-start.1) | copy-done | bytes 2097176
  3.8 0.0 copy-start.2
  3.8 1.2 %copy-done.2 = s32[128,2048]{1,0:T(8,128)S(1)} copy-done((s32[128,2048]{1,0:T(8,128)S(1)}, s32[128,2048]{1,0:T(8,128)}, u32[]{:S(2)}) %copy-start.2) | copy-done | bytes 1048600
  5.0 0.0 copy-start.3
  5.0 0.7 %copy-done.3 = s32[128]{0:T(128)S(1)} copy-done((s32[128]{0:T(128)S(1)}, s32[128]{0:T(128)}, u32[]{:S(2)}) %copy-start.3) | copy-done | bytes 536
  5.7 41.3 %coherence.1 = (f32[2,128,2048]{2,1,0:T(8,128)S(1)}, f32[128,128]{1,0:T(8,128)S(1)}) custom-call(f32[2,128,2048]{2,1,0:T(8,128)S(1)} %copy-done, f32[2,128,2048]{2,1,0:T(8,128)S(1)} %copy-done.1, s32[128,2048]{1,0:T(8,128)S(1)} %copy-done.2, s32[1,128]{1,0:T(1,128)S(1)} %bitcast.1), custom_call_target="tpu_custom_call" | custom-call | tf_op jit(solution)/shard_map/coherence/pallas_call | solution.py:393
  47.0 2.6 %ramp.1 = (f32[2,128,2048]{2,1,0:T(8,128)}, f32[128,2048]{1,0:T(8,128)}) custom-call(f32[2,128,2048]{2,1,0:T(8,128)S(1)} %get-tuple-element.4.gamma, f32[128,128]{1,0:T(8,128)S(1)} %get-tuple-element.5.coefs), custom_call_target="tpu_custom_call" | custom-call | tf_op jit(solution)/shard_map/ramp/pallas_call | solution.py:415
Async XLA Ops:
  0.6 1.6 %copy-start = (f32[2,128,2048]{2,1,0:T(8,128)S(1)}, f32[2,128,2048]{2,1,0:T(8,128)}, u32[]{:S(2)}) copy-start(f32[2,128,2048]{2,1,0:T(8,128)} %lead.1) | copy-start | bytes 6291460
  2.2 1.6 %copy-start.1 = (f32[2,128,2048]{2,1,0:T(8,128)S(1)}, f32[2,128,2048]{2,1,0:T(8,128)}, u32[]{:S(2)}) copy-start(f32[2,128,2048]{2,1,0:T(8,128)} %trail.1) | copy-start | bytes 6291460
  3.8 1.2 %copy-start.2 = (s32[128,2048]{1,0:T(8,128)S(1)}, s32[128,2048]{1,0:T(8,128)}, u32[]{:S(2)}) copy-start(s32[128,2048]{1,0:T(8,128)} %flags.1) | copy-start | bytes 3145732
  5.0 0.7 %copy-start.3 = (s32[128]{0:T(128)S(1)}, s32[128]{0:T(128)}, u32[]{:S(2)}) copy-start(s32[128]{0:T(128)} %param.7) | copy-start | bytes 1540

commit v2 on v1

--- a/solution.py
+++ b/solution.py
@@ -35,10 +35,12 @@
 
 def gamma_kernel(
     count_rows, count_cols,
-    lead, trail, flags, sweep,
+    lead, trail, flags, sweep_in,
     gamma, coefs,
-    first, second, weight, planes, boxed, up_out, down_out, above, below, left_out, right_out, left_in, right_in,
-    side_boxed, side_planes, band, side_band, tri, halo_planes, sums, membership, table, from_cols, table_rows, from_rows,
+    first, second, weight, sweep, planes, up_out, down_out, above, below, left_out, right_out, left_in, right_in,
+    side_boxed, side_planes, corner_planes, band, tri, halo_planes, across_box, across_join,
+    high_in, low_in, join_in, box_in, own_edge, high_edge, low_edge, join_edge, box_edge,
+    sums, membership, table, from_cols, table_rows, from_rows,
     load_sem, row_send, row_recv, col_send, col_recv, ysend, yrecv, rsend, rrecv, token,
 ):
     rows, cols = weight.shape
@@ -84,17 +86,14 @@
     edge_loads = load(0, HALO, 0, cols) + load(inner, rows, 0, cols)
     side_loads = load(HALO, inner, 0, LANES) + load(HALO, inner, cols - LANES, cols)
     step = (inner - HALO) // 3
+    sweep_load = pltpu.make_async_copy(sweep_in, sweep, load_sem.at[len(loads)])
+    sweep_load.start()
+    loads.append(sweep_load)
     main_loads = [load(HALO + i * step, HALO + (i + 1) * step, LANES, cols - LANES) for i in range(3)]
 
     box_row = row_of((rows, 2 * rows))
     box_col = lax.rem(lane_of((rows, 2 * rows)), rows) - box_row
     band[...] = jnp.where((box_col >= -HALO) & (box_col < HALO), 1.0, 0.0).astype(BF16)
-    tall = rows + 2 * HALO
-    side_row = row_of((rows, 2 * tall))
-    side_col = lax.rem(lane_of((rows, 2 * tall)), tall) - side_row
-    side_line = side_col + side_row
-    side_exists = ((side_line >= HALO) | (my_row > 0)) & ((side_line < rows + HALO) | (my_row < count_rows - 1))
-    side_band[...] = jnp.where((side_col >= 0) & (side_col < WIN_R) & side_exists, 1.0, 0.0).astype(BF16)
     tri_row = row_of((2 * HALO, 4 * HALO))
     tri_lane = lane_of((2 * HALO, 4 * HALO))
     tri_col = lax.rem(tri_lane, HALO)
@@ -103,12 +102,15 @@
     tri_above = jnp.where((tri_row < HALO) & (tri_lane < 2 * HALO) & (tri_col >= tri_row), has_above, 0.0)
     tri_below = jnp.where((tri_row >= HALO) & (tri_lane >= 2 * HALO) & (tri_col < tri_row - HALO), has_below, 0.0)
     tri[...] = (tri_above + tri_below).astype(BF16)
-    along = ((my_row * rows + lane_of((LANES, rows))).astype(F32) + 0.5) * (2.0 / (rows * count_rows)) - 1.0
-    burst = row_of((LANES, rows))
-    power = burst // SWEEP_TALLY
-    chosen = jnp.where((burst - power * SWEEP_TALLY == sweep[...]) & (power < 3), 1.0, 0.0)
-    membership[1] = chosen * jnp.where(power == 0, 1.0, jnp.where(power == 1, along, along * along))
-    membership[0] = jnp.transpose(jnp.where(burst == sweep[...], 1.0, 0.0))
+    wide = 2 * LANES
+    from_lane = row_of((wide, wide))
+    to_lane = lane_of((wide, wide))
+    apart = from_lane - to_lane
+    across_box[...] = jnp.where((apart >= -SIDE) & (apart < SIDE), 1.0, 0.0).astype(BF16)
+    from_lane = lax.rem(from_lane, LANES)
+    before = (from_lane >= LANES - SIDE) & (to_lane <= from_lane - (LANES - SIDE))
+    after = (from_lane < SIDE - 1) & (to_lane >= wide - SIDE + 1 + from_lane)
+    across_join[...] = jnp.where(before | after, 1.0, 0.0).astype(BF16)
 
     lane = lane_of((8, LANES))
     lane16 = lane_of((HALO, LANES))
@@ -135,14 +137,7 @@
                 planes[p, pl.ds(row, HALO), here] = high
                 planes[p, pl.ds(rows + row, HALO), here] = low
 
-    arrive(edge_loads)
-    fill(0, up_out)
-    fill(inner, down_out)
-    arrive(side_loads)
-
-    @pl.loop(0, rows // HALO)
-    def _(group):
-        row = pl.multiple_of(group * HALO, HALO)
+    def pack(row):
         packed_left = jnp.zeros((HALO, LANES), F32)
         packed_right = jnp.zeros((HALO, LANES), F32)
         for p, x in enumerate(products(row, 0)):
@@ -153,6 +148,11 @@
         left_out[pl.ds(row, HALO), :] = packed_left
         right_out[pl.ds(row, HALO), :] = packed_right
 
+    arrive(edge_loads)
+    pack(0)
+    pack(inner)
+    fill(0, up_out)
+    fill(inner, down_out)
     pl.semaphore_wait(barrier, len(near))
 
     def send(source, target, send_sem, recv_sem, where):
@@ -162,20 +162,30 @@
         copy.start()
         return copy
 
+    col_copies, corner_copies = [], []
+
+    def send_side(copies, source, target, low, size, to, d_row, d_col):
+        i = len(col_copies) + len(corner_copies)
+        copies.append(
+            send(
+                source.at[pl.ds(low, size), :], target.at[pl.ds(to, size), :],
+                col_send.at[i], col_recv.at[i], at(d_row, d_col),
+            )
+        )
+
+    sides = ((left_out, right_in, -1), (right_out, left_in, 1))
+    for source, target, d_col in sides:
+        send_side(corner_copies, source, target, 0, HALO, rows + HALO, -1, d_col)
+        send_side(corner_copies, source, target, inner, HALO, 0, 1, d_col)
     row_copies = [
         send(up_out, below, row_send.at[0], row_recv.at[0], at(-1, 0)),
         send(down_out, above, row_send.at[1], row_recv.at[1], at(1, 0)),
     ]
-    col_copies = []
-    for source, target, d_col in ((left_out, right_in, -1), (right_out, left_in, 1)):
-        for low, size, to, d_row in ((0, rows, HALO, 0), (0, HALO, rows + HALO, -1), (inner, HALO, 0, 1)):
-            i = len(col_copies)
-            col_copies.append(
-                send(
-                    source.at[pl.ds(low, size), :], target.at[pl.ds(to, size), :],
-                    col_send.at[i], col_recv.at[i], at(d_row, d_col),
-                )
-            )
+    arrive(side_loads)
+    for row in range(HALO, inner, HALO):
+        pack(row)
+    for source, target, d_col in sides:
+        send_side(col_copies, source, target, 0, rows, HALO, 0, d_col)
     for d in (-1, 1):
         signal(token.at[0], at(d, 0))
 
@@ -190,105 +200,130 @@
     for d in (-2, 2):
         signal(token.at[1], at(d, 0))
 
-    wide = 2 * LANES
-    for p in range(4):
-        @pl.loop(0, cols // wide)
-        def _(n):
-            here = pl.ds(pl.multiple_of(n * wide, wide), wide)
-            boxed[p, :, here] = jnp.dot(band[...], planes[p, :, here], preferred_element_type=F32)
+    tiles = cols // wide
+    for n in range(tiles):
+        there = pl.ds(n * wide, wide)
+        for p in range(4):
+            box = jnp.dot(band[...], planes[p, :, there], preferred_element_type=F32)
+            high, low = split_pair(box[HALO:inner])
+            high_in[n, p] = high
+            low_in[n, p] = low
+            own_edge[p, pl.ds(0, HALO), there] = box[:HALO]
+            own_edge[p, pl.ds(HALO, HALO), there] = box[inner:]
+
+    sweep_load.wait()
+    along = ((my_row * rows + lane_of((LANES, rows))).astype(F32) + 0.5) * (2.0 / (rows * count_rows)) - 1.0
+    burst = row_of((LANES, rows))
+    power = burst // SWEEP_TALLY
+    chosen = jnp.where((burst - power * SWEEP_TALLY == sweep[...]) & (power < 3), 1.0, 0.0)
+    membership[1] = chosen * jnp.where(power == 0, 1.0, jnp.where(power == 1, along, along * along))
+    membership[0] = jnp.transpose(jnp.where(burst == sweep[...], 1.0, 0.0))
 
     for copy in col_copies:
         copy.wait()
-    for i, (arrived, exists) in enumerate(((left_in, my_col > 0), (right_in, my_col < count_cols - 1))):
-        high, low = split_pair(arrived[...] * jnp.where(exists, 1.0, 0.0))
-        side_planes[pl.ds(0, tall), pl.ds(i * LANES, LANES)] = high
-        side_planes[pl.ds(tall, tall), pl.ds(i * LANES, LANES)] = low
-    side_boxed[...] = jnp.dot(side_band[...], side_planes[...], preferred_element_type=F32)
+    side_exists = [jnp.where(my_col > 0, 1.0, 0.0), jnp.where(my_col < count_cols - 1, 1.0, 0.0)]
+    for i, arrived in enumerate((left_in, right_in)):
+        there = pl.ds(i * LANES, LANES)
+        high, low = split_pair(arrived[pl.ds(HALO, rows), :] * side_exists[i])
+        side_planes[pl.ds(0, rows), there] = high
+        side_planes[pl.ds(rows, rows), there] = low
+    side_boxed[...] = jnp.dot(band[...], side_planes[...], preferred_element_type=F32)
+
+    def join(high_ref, low_ref, join_ref, count, side_lines):
+        first_half = lane_of((count, LANES)) < LANES // 2
+        parts = [high_ref, low_ref]
+        for p in range(4):
+            packed = side_lines()
+            left = split_pair(pltpu.roll(packed[:, :LANES], LANES - SIDE * (p + 1), 1))
+            right = packed[:, LANES:]
+            right = split_pair(right if p == 0 else pltpu.roll(right, LANES - SIDE * p, 1))
+            for n in range(tiles):
+                for i in range(2):
+                    before = left[i] if n == 0 else parts[i][n - 1, p, :, pl.ds(LANES, LANES)]
+                    after = right[i] if n == tiles - 1 else parts[i][n + 1, p, :, pl.ds(0, LANES)]
+                    join_ref[n, p, :, pl.ds(i * LANES, LANES)] = jnp.where(first_half, after, before)
+
+    def box_across(high_ref, low_ref, join_ref, box_ref, count, n):
+        lines = 4 * count
+        total = jnp.dot(high_ref[n].reshape(lines, wide), across_box[...], preferred_element_type=F32)
+        total += jnp.dot(low_ref[n].reshape(lines, wide), across_box[...], preferred_element_type=F32)
+        total += jnp.dot(join_ref[n].reshape(lines, wide), across_join[...], preferred_element_type=F32)
+        box_ref[n] = total.reshape(4, count, wide)
+
+    between = inner - HALO
+    join(high_in, low_in, join_in, between, lambda: side_boxed[pl.ds(HALO, between), :])
+
+    for n in range(tiles):
+        box_across(high_in, low_in, join_in, box_in, between, n)
 
     across_first = ((my_col * cols + lane).astype(F32) + 0.5) * (2.0 / (cols * count_cols)) - 1.0
 
-    def finish(group):
-        here = pl.ds(pl.multiple_of(group * 8, 8), 8)
-        packed = side_boxed[here, pl.ds(0, LANES)], side_boxed[here, pl.ds(LANES, LANES)]
-
-        def block(p, j):
-            if j == 0:
-                return pltpu.roll(packed[0], LANES - SIDE * (p + 1), 1)
-            if j == blocks + 1:
-                return packed[1] if p == 0 else pltpu.roll(packed[1], LANES - SIDE * p, 1)
-            return boxed[p, here, pl.ds((j - 1) * LANES, LANES)]
-
-        one, one_turned, two, two_turned, four_turned = ({} for _ in range(5))
-        raw, raw_turned = {}, {}
+    def finish(box_ref, at_row, row):
+        here = pl.ds(row, 8)
         totals = [jnp.zeros((8, LANES), F32) for _ in range(7)]
-        for j in range(blocks + 2):
-            for p in range(4):
-                raw[p, j] = block(p, j)
-                raw_turned[p, j] = pltpu.roll(raw[p, j], LANES - 1, 1)
-                ready = [j - 1] if j else []
-                if j == blocks + 1:
-                    ready.append(j)
-                for k in ready:
-                    follow = raw_turned[p, min(k + 1, j)]
-                    one[p, k] = raw[p, k] + jnp.where(lane < LANES - 1, raw_turned[p, k], follow)
-                    one_turned[p, k] = pltpu.roll(one[p, k], LANES - 2, 1)
-                    if k:
-                        i = k - 1
-                        two[p, i] = one[p, i] + jnp.where(lane < LANES - 2, one_turned[p, i], one_turned[p, k])
-                        two_turned[p, i] = pltpu.roll(two[p, i], SIDE, 1)
-            done = [j - 2] if j >= 3 else []
-            if j == blocks + 1:
-                done.append(j - 1)
-            for i in done:
-                real, imag, power_a, power_b = (
-                    two[p, i] + jnp.where(lane >= SIDE, two_turned[p, i], two_turned[p, i - 1]) for p in range(4)
-                )
-                scale = lax.rsqrt((power_a + 1.0) * (power_b + 1.0))
-                real, imag = real * scale, imag * scale
-                there = pl.ds((i - 1) * LANES, LANES)
-                gamma[0, here, there] = real
-                gamma[1, here, there] = imag
-                w = weight[here, there].astype(F32)
-                across = across_first + (i - 1) * (LANES * 2.0 / (cols * count_cols))
-                wu = w * across
-                terms = (w, wu, wu * across, w * real, w * imag, wu * real, wu * imag)
-                totals = [total + term for total, term in zip(totals, terms)]
+        for j in range(blocks):
+            half = pl.ds(j % 2 * LANES, LANES)
+            real, imag, power_a, power_b = (box_ref[j // 2, p, pl.ds(at_row, 8), half] for p in range(4))
+            scale = lax.rsqrt((power_a + 1.0) * (power_b + 1.0))
+            real, imag = real * scale, imag * scale
+            there = pl.ds(j * LANES, LANES)
+            gamma[0, here, there] = real
+            gamma[1, here, there] = imag
+            w = weight[here, there].astype(F32)
+            across = across_first + j * (LANES * 2.0 / (cols * count_cols))
+            wu = w * across
+            terms = (w, wu, wu * across, w * real, w * imag, wu * real, wu * imag)
+            totals = [total + term for total, term in zip(totals, terms)]
+        line = jnp.zeros((8, LANES), F32)
         for q, total in enumerate(totals):
-            sums[here, pl.ds(q * LANES, LANES)] = total
-
-    @pl.loop(HALO // 8, inner // 8)
+            line = jnp.where(lane == q, jnp.sum(total, axis=1, keepdims=True), line)
+        sums[here, :] = line
+
+    @pl.loop(0, between // 8)
     def _(group):
-        finish(group)
+        at_row = pl.multiple_of(group * 8, 8)
+        finish(box_in, at_row, pl.multiple_of(at_row + HALO, 8))
 
     pl.semaphore_wait(token.at[1], 2)
     for d in (-4, 4):
         signal(token.at[2], at(d, 0))
 
-    for copy in row_copies:
+    for copy in corner_copies + row_copies:
         copy.wait()
+    for i, arrived in enumerate((left_in, right_in)):
+        there = pl.ds(i * LANES, LANES)
+        for k, to in enumerate((0, rows + HALO)):
+            high, low = split_pair(arrived[pl.ds(to, HALO), :] * side_exists[i])
+            corner_planes[pl.ds(2 * k * HALO, HALO), there] = high
+            corner_planes[pl.ds((2 * k + 1) * HALO, HALO), there] = low
+    side_edge = jnp.dot(tri[...], corner_planes[...], preferred_element_type=F32)
+    side_edge += jnp.concatenate([side_boxed[pl.ds(0, HALO), :], side_boxed[pl.ds(inner, HALO), :]], axis=0)
     for p in range(4):
         for i, arrived in enumerate((above, below)):
             high, low = split_pair(arrived[p])
             halo_planes[p, pl.ds(2 * i * HALO, HALO), :] = high
             halo_planes[p, pl.ds((2 * i + 1) * HALO, HALO), :] = low
-
-        @pl.loop(0, cols // wide)
-        def _(n):
-            there = pl.ds(pl.multiple_of(n * wide, wide), wide)
+    for n in range(tiles):
+        there = pl.ds(n * wide, wide)
+        for p in range(4):
             extra = jnp.dot(tri[...], halo_planes[p, :, there], preferred_element_type=F32)
-            boxed[p, pl.ds(0, HALO), there] += extra[:HALO]
-            boxed[p, pl.ds(inner, HALO), there] += extra[HALO:]
-
-    @pl.loop(0, 2 * HALO // 8)
-    def _(i):
-        finish(jnp.where(i < HALO // 8, i, i + (inner - HALO) // 8))
-
-    by_burst = jnp.dot(membership[1], sums[...], preferred_element_type=F32, precision=EXACT)
-    kind = lane_of((8, 7 * LANES)) // LANES
-    pick = jnp.where(kind == row_of((8, 7 * LANES)), 1.0, 0.0)
-    table[...] = lax.dot_general(
-        pick, by_burst, (((1,), (1,)), ((), ())), preferred_element_type=F32, precision=EXACT
+            high, low = split_pair(own_edge[p, :, there] + extra)
+            high_edge[n, p] = high
+            low_edge[n, p] = low
+    join(
+        high_edge, low_edge, join_edge, 2 * HALO,
+        lambda: side_edge,
     )
+    for n in range(tiles):
+        box_across(high_edge, low_edge, join_edge, box_edge, 2 * HALO, n)
+    for group in range(2 * HALO // 8):
+        at_row = group * 8
+        finish(box_edge, at_row, at_row if at_row < HALO else at_row - HALO + inner)
+
+    full = lax.dot_general(
+        jnp.transpose(sums[...])[:8], membership[1], (((1,), (1,)), ((), ())), preferred_element_type=F32, precision=EXACT
+    )
+    table[...] = full[:4] + pltpu.roll(full[4:], LANES // 2, 1)
 
     copies = [
         send(table, from_cols.at[k - 1], ysend.at[k - 1], yrecv.at[k - 1], at(0, k)) for k in range(1, 4)
@@ -307,6 +342,7 @@
     for i in range(len(distances)):
         total = total + from_rows[i]
 
+    total = jnp.concatenate([total, pltpu.roll(total, LANES // 2, 1)], axis=0)
     once = pltpu.roll(total, LANES - SWEEP_TALLY, 1)
     twice = pltpu.roll(total, LANES - 2 * SWEEP_TALLY, 1)
     count, sum_u, sum_uu, h0_re, h0_im, hu_re, hu_im = (total[q:q + 1] for q in range(7))
@@ -386,6 +422,8 @@
 def on_device(count_rows, count_cols, lead, trail, flags, sweep):
     rows, cols = flags.shape
     tall = rows + 2 * HALO
+    wide = 2 * LANES
+    tiles, between = cols // wide, rows - 2 * HALO
     vmem = pl.BlockSpec(memory_space=pltpu.VMEM)
     hbm = pl.BlockSpec(memory_space=pl.ANY)
     dma = pltpu.SemaphoreType.DMA
@@ -393,22 +431,28 @@
     gamma, coefs = pl.pallas_call(
         functools.partial(gamma_kernel, count_rows, count_cols),
         out_shape=(V((2, rows, cols), F32), V((rows, LANES), F32)),
-        in_specs=[hbm, hbm, hbm, vmem],
+        in_specs=[hbm, hbm, hbm, hbm],
         out_specs=(vmem, vmem),
         scratch_shapes=[
-            V((2, rows, cols), F32), V((2, rows, cols), F32), V((rows, cols), jnp.int32),
-            V((4, 2 * rows, cols), BF16), V((4, rows, cols), F32),
+            V((2, rows, cols), F32), V((2, rows, cols), F32), V((rows, cols), jnp.int32), V((1, rows), jnp.int32),
+            V((4, 2 * rows, cols), BF16),
             V((4, HALO, cols), F32), V((4, HALO, cols), F32), V((4, HALO, cols), F32), V((4, HALO, cols), F32),
             V((rows, LANES), F32), V((rows, LANES), F32), V((tall, LANES), F32), V((tall, LANES), F32),
-            V((rows, 2 * LANES), F32), V((2 * tall, 2 * LANES), BF16),
-            V((rows, 2 * rows), BF16), V((rows, 2 * tall), BF16), V((2 * HALO, 4 * HALO), BF16),
-            V((4, 4 * HALO, cols), BF16), V((rows, 7 * LANES), F32), V((2, LANES, rows), F32),
-            V((8, LANES), F32), V((3, 8, LANES), F32), V((8, LANES), F32), V((2 * REACH, 8, LANES), F32),
-            dma((21,)), dma((2,)), dma((2,)), dma((6,)), dma((6,)), dma((3,)), dma((3,)),
+            V((rows, 2 * LANES), F32), V((2 * rows, 2 * LANES), BF16), V((4 * HALO, 2 * LANES), BF16),
+            V((rows, 2 * rows), BF16), V((2 * HALO, 4 * HALO), BF16),
+            V((4, 4 * HALO, cols), BF16), V((wide, wide), BF16), V((wide, wide), BF16),
+            V((tiles, 4, between, wide), BF16), V((tiles, 4, between, wide), BF16),
+            V((tiles, 4, between, wide), BF16), V((tiles, 4, between, wide), F32),
+            V((4, 2 * HALO, cols), F32),
+            V((tiles, 4, 2 * HALO, wide), BF16), V((tiles, 4, 2 * HALO, wide), BF16),
+            V((tiles, 4, 2 * HALO, wide), BF16), V((tiles, 4, 2 * HALO, wide), F32),
+            V((rows, LANES), F32), V((2, LANES, rows), F32),
+            V((4, LANES), F32), V((3, 4, LANES), F32), V((4, LANES), F32), V((2 * REACH, 4, LANES), F32),
+            dma((22,)), dma((2,)), dma((2,)), dma((6,)), dma((6,)), dma((3,)), dma((3,)),
             dma((2 * REACH,)), dma((2 * REACH,)), pltpu.SemaphoreType.REGULAR((3,)),
         ],
         compiler_params=pltpu.CompilerParams(
-            collective_id=0, has_side_effects=True, vmem_limit_bytes=40 * 1024 * 1024
+            collective_id=0, has_side_effects=True, vmem_limit_bytes=64_000_000
         ),
         name="coherence",
     )(lead, trail, flags, sweep.reshape(1, rows))

time: 49.8 us -> 32.9 us (0.66)
  Pallas kernels: 43.9 us -> 32.2 us
  local copies, waits for them, and re-layouts: 5.05 us -> 0 us
    pallas_call x1, Pallas kernels: 41.3 us -> 29.6 us  [on_device(): pl.pallas_call(functools.partial(gamma_kernel, count_rows, count_cols), o...]
    unnamed x8 -> x0, local copies, waits for them, and re-layouts: 5.05 us -> none
where the time goes in v2:
time: 32.9 us; the launch traced here: 32.8 us
  Pallas kernels  32.2 us (98%)
  between operations  0.64 us (2%)
    pallas_call x1, Pallas kernels, on_device(): pl.pallas_call(functools.partial(gamma_kernel, count_rows, count_cols), o...  29.6 us
    pallas_call x1, Pallas kernels, on_device(): pl.pallas_call(functools.partial(ramp_kernel, count_rows, count_cols), ou...  2.61 us

profile of v2, /device:TPU:1, one launch (start us, length us, event | category | flops | bytes accessed | tf_op | source)
XLA Modules:
  0.0 32.8 jit_solution(18153048593776327224)
XLA Ops:
  0.6 29.6 %coherence.1 = (f32[2,128,2048]{2,1,0:T(8,128)S(1)}, f32[128,128]{1,0:T(8,128)S(1)}) custom-call(f32[2,128,2048]{2,1,0:T(8,128)} %lead.1, f32[2,128,2048]{2,1,0:T(8,128)} %trail.1, s32[128,2048]{1,0:T(8,128)} %flags.1, s32[1,128]{1,0:T(1,128)} %bitcast.1), custom_call_target="tpu_custom_call" | custom-call | tf_op jit(solution)/shard_map/coherence/pallas_call | solution.py:431
  30.2 2.6 %ramp.1 = (f32[2,128,2048]{2,1,0:T(8,128)}, f32[128,2048]{1,0:T(8,128)}) custom-call(f32[2,128,2048]{2,1,0:T(8,128)S(1)} %get-tuple-element.4.gamma, f32[128,128]{1,0:T(8,128)S(1)} %get-tuple-element.5.coefs), custom_call_target="tpu_custom_call" | custom-call | tf_op jit(solution)/shard_map/ramp/pallas_call | solution.py:459

commit v3 on v2

v3 whole, which is shorter than its diff:
```python
import functools

import jax
import jax.numpy as jnp
from jax import lax
from jax.experimental import pallas as pl
from jax.experimental.pallas import tpu as pltpu
from jax.sharding import PartitionSpec as P

WIN_R = 32
WIN_C = 8
SWEEP_TALLY = 16
HALO = WIN_R // 2
SIDE = WIN_C // 2
LANES = 128
REACH = 8
PARTS = 4
MESH = pl.DeviceIdType.MESH
F32 = jnp.float32
BF16 = jnp.bfloat16
EXACT = lax.Precision.HIGHEST


def split_pair(x):
    high = x.astype(BF16)
    return high, (x - high.astype(F32)).astype(BF16)


def lane_of(shape):
    return lax.broadcasted_iota(jnp.int32, shape, 1)


def row_of(shape):
    return lax.broadcasted_iota(jnp.int32, shape, 0)


def gamma_kernel(
    count_rows, count_cols,
    lead, trail, flags, sweep_in,
    gamma, size, coefs,
    first, second, weight, sweep, planes, up_out, down_out, above, below, left_out, right_out, left_in, right_in,
    side_boxed, side_edge, side_planes, corner_planes, band, tri, halo_planes, across_box, across_join,
    high_in, low_in, join_in, box_in, own_edge, high_edge, low_edge, join_edge, box_edge,
    line_in, line_edge, sums, membership, table, from_cols, table_rows, from_rows,
    load_sem, row_send, row_recv, col_send, col_recv, ysend, yrecv, rsend, rrecv, token,
):
    rows, cols = weight.shape
    blocks = cols // LANES
    my_row = lax.axis_index("rows")
    my_col = lax.axis_index("cols")

    def at(d_row, d_col):
        return {
            "rows": lax.rem(my_row + d_row + count_rows, count_rows),
            "cols": lax.rem(my_col + d_col + count_cols, count_cols),
        }

    def signal(sem, where):
        pl.semaphore_signal(sem, inc=1, device_id=where, device_id_type=MESH)

    barrier = pltpu.get_barrier_semaphore()
    def exists(d_row):
        return my_row >= -d_row if d_row < 0 else my_row < count_rows - d_row

    def if_row(d_row, act):
        if d_row:
            pl.when(exists(d_row))(act)
        else:
            act()

    def number(*d_rows):
        return sum(exists(d).astype(jnp.int32) for d in d_rows)

    for a in (-1, 0, 1):
        for b in (-1, 0, 1) if a else (-1, 1, 2):
            if_row(a, lambda a=a, b=b: signal(barrier, at(a, b)))

    loads = []

    def load(low, high, left, right):
        started = []
        window = (pl.ds(low, high - low), pl.ds(left, right - left))
        for source, target in ((lead, first), (trail, second)):
            started.append((source.at[(slice(None),) + window], target.at[(slice(None),) + window]))
        started.append((flags.at[window], weight.at[window]))
        copies = []
        for source, target in started:
            copy = pltpu.make_async_copy(source, target, load_sem.at[len(loads)])
            copy.start()
            loads.append(copy)
            copies.append(copy)
        return copies

    def arrive(copies):
        for copy in copies:
            copy.wait()

    inner = rows - HALO
    part = cols // PARTS
    edge_loads = []
    for c in range(PARTS):
        right = (c + 1) * part - (LANES if c == PARTS - 1 else 0)
        edge_loads.append(load(0, HALO, c * part, right) + load(inner, rows, c * part, right))
        if c == 0:
            edge_loads[0] += load(0, HALO, cols - LANES, cols) + load(inner, rows, cols - LANES, cols)
    side_loads = load(HALO, inner, 0, LANES) + load(HALO, inner, cols - LANES, cols)
    step = (inner - HALO) // 3
    sweep_load = pltpu.make_async_copy(sweep_in, sweep, load_sem.at[len(loads)])
    sweep_load.start()
    loads.append(sweep_load)
    main_loads = [load(HALO + i * step, HALO + (i + 1) * step, LANES, cols - LANES) for i in range(3)]

    lane = lane_of((8, LANES))
    lane16 = lane_of((HALO, LANES))

    def products(row, block, sends=None):
        here = (pl.ds(row, HALO), pl.ds(block * LANES, LANES))
        w = weight[here].astype(F32)
        real_a, imag_a = first[(0,) + here] * w, first[(1,) + here] * w
        real_b, imag_b = second[(0,) + here] * w, second[(1,) + here] * w
        if sends is not None:
            top = jnp.maximum(jnp.abs(real_b), jnp.abs(imag_b))
            some = top > 0.0
            unit = 1.0 / jnp.where(some, top, 1.0)
            x, y = jnp.where(some, real_b * unit, 1.0), imag_b * unit
            square = x * x + y * y
            turn = lax.rsqrt(square)
            there = here[1]
            sends[0, :, there] = (real_a * x + imag_a * y) * turn
            sends[1, :, there] = (imag_a * x - real_a * y) * turn
            sends[2, :, there] = top * (square * turn)
        return (
            real_a * real_b + imag_a * imag_b,
            imag_a * real_b - real_a * imag_b,
            real_a * real_a + imag_a * imag_a,
            real_b * real_b + imag_b * imag_b,
        )

    def fill(row, sends=None, some=range(blocks)):
        for block in some:
            here = pl.ds(block * LANES, LANES)
            for p, x in enumerate(products(row, block, sends)):
                high, low = split_pair(x)
                planes[p, pl.ds(row, HALO), here] = high
                planes[p, pl.ds(rows + row, HALO), here] = low

    def pack(row):
        packed_left = jnp.zeros((HALO, LANES), F32)
        packed_right = jnp.zeros((HALO, LANES), F32)
        for p, x in enumerate(products(row, 0)):
            x = jnp.where(lane16 < SIDE, x, 0.0)
            packed_left += x if p == 0 else pltpu.roll(x, SIDE * p, 1)
        for p, x in enumerate(products(row, blocks - 1)):
            packed_right += pltpu.roll(jnp.where(lane16 >= LANES - SIDE, x, 0.0), SIDE * (p + 1), 1)
        left_out[pl.ds(row, HALO), :] = packed_left
        right_out[pl.ds(row, HALO), :] = packed_right

    def send(source, target, send_sem, recv_sem, d_row, d_col):
        copy = pltpu.make_async_remote_copy(
            src_ref=source, dst_ref=target, send_sem=send_sem, recv_sem=recv_sem,
            device_id=at(d_row, d_col), device_id_type=MESH,
        )
        if_row(d_row, copy.start)
        return copy, d_row

    def finish_send(sent):
        copy, d_row = sent
        if_row(-d_row, copy.wait_recv)
        if_row(d_row, copy.wait_send)

    @pl.when(my_row == 0)
    def _():
        above[...] = jnp.zeros_like(above)
        for arrived in (left_in, right_in):
            arrived[pl.ds(0, HALO), :] = jnp.zeros((HALO, LANES), F32)

    @pl.when(my_row == count_rows - 1)
    def _():
        below[...] = jnp.zeros_like(below)
        for arrived in (left_in, right_in):
            arrived[pl.ds(rows + HALO, HALO), :] = jnp.zeros((HALO, LANES), F32)

    distances = [d for k in range(REACH, 0, -1) for d in (-k, k)]
    for i, d in enumerate(distances):
        @pl.when(jnp.logical_not(exists(-d)))
        def _(i=i):
            from_rows[i] = jnp.zeros((4, LANES), F32)

    col_copies, corner_copies, row_copies = [], [], []

    def send_side(copies, source, target, low, count, to, d_row, d_col):
        i = len(col_copies) + len(corner_copies)
        copies.append(
            send(
                source.at[pl.ds(low, count), :], target.at[pl.ds(to, count), :],
                col_send.at[i], col_recv.at[i], d_row, d_col,
            )
        )

    sides = ((left_out, right_in, -1), (right_out, left_in, 1))
    for c in range(PARTS):
        arrive(edge_loads[c])
        if c == 0:
            pack(0)
            pack(inner)
        some = range(c * part // LANES, (c + 1) * part // LANES)
        fill(0, up_out, some)
        fill(inner, down_out, some)
        if c == 0:
            pl.semaphore_wait(barrier, 3 + 3 * number(-1, 1))
            for source, target, d_col in sides:
                send_side(corner_copies, source, target, 0, HALO, rows + HALO, -1, d_col)
                send_side(corner_copies, source, target, inner, HALO, 0, 1, d_col)
        there = pl.ds(c * part, part)
        row_copies.append([
            send(
                source.at[:, :, there], target.at[:, :, there],
                row_send.at[2 * c + i], row_recv.at[2 * c + i], d_row, 0,
            )
            for i, (source, target, d_row) in enumerate(((up_out, below, -1), (down_out, above, 1)))
        ])
    arrive(side_loads)
    for row in range(HALO, inner, HALO):
        pack(row)
    for source, target, d_col in sides:
        send_side(col_copies, source, target, 0, rows, HALO, 0, d_col)
    for d in (-1, 1):
        if_row(d, lambda d=d: signal(token.at[0], at(d, 0)))

    box_row = row_of((rows, 2 * rows))
    box_col = lax.rem(lane_of((rows, 2 * rows)), rows) - box_row
    band[...] = jnp.where((box_col >= -HALO) & (box_col < HALO), 1.0, 0.0).astype(BF16)
    tri_row = row_of((2 * HALO, 4 * HALO))
    tri_lane = lane_of((2 * HALO, 4 * HALO))
    tri_col = lax.rem(tri_lane, HALO)
    has_above = jnp.where(my_row > 0, 1.0, 0.0)
    has_below = jnp.where(my_row < count_rows - 1, 1.0, 0.0)
    tri_above = jnp.where((tri_row < HALO) & (tri_lane < 2 * HALO) & (tri_col >= tri_row), has_above, 0.0)
    tri_below = jnp.where((tri_row >= HALO) & (tri_lane >= 2 * HALO) & (tri_col < tri_row - HALO), has_below, 0.0)
    tri[...] = (tri_above + tri_below).astype(BF16)
    wide = 2 * LANES
    from_lane = row_of((wide, wide))
    to_lane = lane_of((wide, wide))
    apart = from_lane - to_lane
    across_box[...] = jnp.where((apart >= -SIDE) & (apart < SIDE), 1.0, 0.0).astype(BF16)
    from_lane = lax.rem(from_lane, LANES)
    before = (from_lane >= LANES - SIDE) & (to_lane <= from_lane - (LANES - SIDE))
    after = (from_lane < SIDE - 1) & (to_lane >= wide - SIDE + 1 + from_lane)
    across_join[...] = jnp.where(before | after, 1.0, 0.0).astype(BF16)

    for i, copies in enumerate(main_loads):
        arrive(copies)

        @pl.loop(HALO + i * step, HALO + (i + 1) * step, step=HALO)
        def _(row):
            fill(pl.multiple_of(row, HALO))

    tiles = cols // wide
    for n in range(tiles):
        there = pl.ds(n * wide, wide)
        for p in range(4):
            box = jnp.dot(band[...], planes[p, :, there], preferred_element_type=F32)
            high, low = split_pair(box[HALO:inner])
            high_in[n, p] = high
            low_in[n, p] = low
            own_edge[p, pl.ds(0, HALO), there] = box[:HALO]
            own_edge[p, pl.ds(HALO, HALO), there] = box[inner:]

    sweep_load.wait()
    along = ((my_row * rows + lane_of((LANES, rows))).astype(F32) + 0.5) * (2.0 / (rows * count_rows)) - 1.0
    burst = row_of((LANES, rows))
    power = burst // SWEEP_TALLY
    chosen = jnp.where((burst - power * SWEEP_TALLY == sweep[...]) & (power < 3), 1.0, 0.0)
    membership[1] = chosen * jnp.where(power == 0, 1.0, jnp.where(power == 1, along, along * along))
    membership[0] = jnp.transpose(jnp.where(burst == sweep[...], 1.0, 0.0))

    def join(high_ref, low_ref, join_ref, count, n, packed):
        first_half = lane_of((count, LANES)) < LANES // 2
        parts = [high_ref, low_ref]
        for p in range(4):
            if n == 0:
                outer = split_pair(pltpu.roll(packed[:, :LANES], LANES - SIDE * (p + 1), 1))
            elif n == tiles - 1:
                outer = packed[:, LANES:]
                outer = split_pair(outer if p == 0 else pltpu.roll(outer, LANES - SIDE * p, 1))
            for i in range(2):
                before = outer[i] if n == 0 else parts[i][n - 1, p, :, pl.ds(LANES, LANES)]
                after = outer[i] if n == tiles - 1 else parts[i][n + 1, p, :, pl.ds(0, LANES)]
                join_ref[n, p, :, pl.ds(i * LANES, LANES)] = jnp.where(first_half, after, before)

    def box_across(high_ref, low_ref, join_ref, box_ref, count, n):
        lines = 4 * count
        total = jnp.dot(high_ref[n].reshape(lines, wide), across_box[...], preferred_element_type=F32)
        total += jnp.dot(low_ref[n].reshape(lines, wide), across_box[...], preferred_element_type=F32)
        total += jnp.dot(join_ref[n].reshape(lines, wide), across_join[...], preferred_element_type=F32)
        box_ref[n] = total.reshape(4, count, wide)

    across_first = ((my_col * cols + lane).astype(F32) + 0.5) * (2.0 / (cols * count_cols)) - 1.0

    def finish(box_ref, line_ref, n, at_row, row, fresh):
        here = pl.ds(row, 8)
        totals = None if fresh else [line_ref[q, pl.ds(at_row, 8), :] for q in range(7)]
        for j in (2 * n, 2 * n + 1):
            half = pl.ds(j % 2 * LANES, LANES)
            real, imag, power_a, power_b = (box_ref[n, p, pl.ds(at_row, 8), half] for p in range(4))
            scale = lax.rsqrt((power_a + 1.0) * (power_b + 1.0))
            real, imag = real * scale, imag * scale
            there = pl.ds(j * LANES, LANES)
            gamma[0, here, there] = real
            gamma[1, here, there] = imag
            w = weight[here, there].astype(F32)
            across = across_first + j * (LANES * 2.0 / (cols * count_cols))
            wu = w * across
            terms = (w, wu, wu * across, w * real, w * imag, wu * real, wu * imag)
            totals = list(terms) if totals is None else [total + term for total, term in zip(totals, terms)]
        for q, total in enumerate(totals):
            line_ref[q, pl.ds(at_row, 8), :] = total

    def gather_lines(line_ref, at_row, row):
        line = jnp.zeros((8, LANES), F32)
        for q in range(7):
            line = jnp.where(lane == q, jnp.sum(line_ref[q, pl.ds(at_row, 8), :], axis=1, keepdims=True), line)
        sums[pl.ds(row, 8), :] = line

    between = inner - HALO

    def run_inner(order, fresh_at, packed=None):
        waiting = None
        for n in order + [None]:
            if n is not None:
                join(high_in, low_in, join_in, between, n, packed)
                box_across(high_in, low_in, join_in, box_in, between, n)
            if waiting is not None:
                for at_row in range(0, between, 8):
                    finish(box_in, line_in, waiting, at_row, at_row + HALO, waiting == fresh_at)
            waiting = n

    run_inner(list(range(1, tiles - 1)), 1)

    pl.semaphore_wait(token.at[0], number(-1, 1))
    for d in (-2, 2):
        if_row(d, lambda d=d: signal(token.at[1], at(d, 0)))

    for sent in col_copies:
        finish_send(sent)
    side_exists = [jnp.where(my_col > 0, 1.0, 0.0), jnp.where(my_col < count_cols - 1, 1.0, 0.0)]
    for i, arrived in enumerate((left_in, right_in)):
        there = pl.ds(i * LANES, LANES)
        high, low = split_pair(arrived[pl.ds(HALO, rows), :] * side_exists[i])
        side_planes[pl.ds(0, rows), there] = high
        side_planes[pl.ds(rows, rows), there] = low
    side_boxed[...] = jnp.dot(band[...], side_planes[...], preferred_element_type=F32)
    run_inner([0, tiles - 1], None, side_boxed[pl.ds(HALO, between), :])
    for at_row in range(0, between, 8):
        gather_lines(line_in, at_row, at_row + HALO)

    for sent in corner_copies:
        finish_send(sent)
    for i, arrived in enumerate((left_in, right_in)):
        there = pl.ds(i * LANES, LANES)
        for k, to in enumerate((0, rows + HALO)):
            high, low = split_pair(arrived[pl.ds(to, HALO), :] * side_exists[i])
            corner_planes[pl.ds(2 * k * HALO, HALO), there] = high
            corner_planes[pl.ds((2 * k + 1) * HALO, HALO), there] = low
    side_edge[...] = jnp.dot(tri[...], corner_planes[...], preferred_element_type=F32) + jnp.concatenate(
        [side_boxed[pl.ds(0, HALO), :], side_boxed[pl.ds(inner, HALO), :]], axis=0
    )

    ready = 0
    for c in range(PARTS):
        for sent in row_copies[c]:
            finish_send(sent)
        if c == 0:
            pl.semaphore_wait(token.at[1], number(-2, 2))
            for d in (-4, 4):
                if_row(d, lambda d=d: signal(token.at[2], at(d, 0)))
        here = pl.ds(c * part, part)
        for i, arrived in enumerate((above, below)):
            turned_re, turned_im, length = (arrived[q, :, here] for q in range(3))
            arrived_planes = (
                turned_re * length, turned_im * length, turned_re * turned_re + turned_im * turned_im, length * length
            )
            for p, x in enumerate(arrived_planes):
                high, low = split_pair(x)
                halo_planes[p, pl.ds(2 * i * HALO, HALO), here] = high
                halo_planes[p, pl.ds((2 * i + 1) * HALO, HALO), here] = low
        last = (c + 1) * part // wide
        for n in range(c * part // wide, last):
            there = pl.ds(n * wide, wide)
            for p in range(4):
                extra = jnp.dot(tri[...], halo_planes[p, :, there], preferred_element_type=F32)
                high, low = split_pair(own_edge[p, :, there] + extra)
                high_edge[n, p] = high
                low_edge[n, p] = low
        until = last if last == tiles else last - 1
        for n in range(ready, until):
            join(high_edge, low_edge, join_edge, 2 * HALO, n, side_edge[...])
            box_across(high_edge, low_edge, join_edge, box_edge, 2 * HALO, n)
        for n in range(ready, until):
            for at_row in range(0, 2 * HALO, 8):
                finish(box_edge, line_edge, n, at_row, at_row if at_row < HALO else at_row - HALO + inner, n == 0)
        ready = until
    for at_row in range(0, 2 * HALO, 8):
        gather_lines(line_edge, at_row, at_row if at_row < HALO else at_row - HALO + inner)

    full = lax.dot_general(
        jnp.transpose(sums[...])[:8], membership[1], (((1,), (1,)), ((), ())), preferred_element_type=F32, precision=EXACT
    )
    table[...] = full[:4] + pltpu.roll(full[4:], LANES // 2, 1)

    copies = [
        send(table, from_cols.at[k - 1], ysend.at[k - 1], yrecv.at[k - 1], 0, k) for k in (2, 1, 3)
    ]
    pl.semaphore_wait(token.at[2], number(-4, 4))
    for sent in copies:
        finish_send(sent)
    table_rows[...] = (table[...] + from_cols[0]) + (from_cols[1] + from_cols[2])
    copies = [
        send(table_rows, from_rows.at[i], rsend.at[i], rrecv.at[i], d, 0) for i, d in enumerate(distances)
    ]

    @pl.loop(0, rows // 8)
    def _(group):
        here = pl.ds(pl.multiple_of(group * 8, 8), 8)
        for j in range(blocks):
            there = pl.ds(j * LANES, LANES)
            real, imag = gamma[0, here, there], gamma[1, here, there]
            size[here, there] = jnp.sqrt(real * real + imag * imag)

    for sent in copies:
        finish_send(sent)
    total = table_rows[...]
    for i in range(len(distances)):
        total = total + from_rows[i]

    total = jnp.concatenate([total, pltpu.roll(total, LANES // 2, 1)], axis=0)
    once = pltpu.roll(total, LANES - SWEEP_TALLY, 1)
    twice = pltpu.roll(total, LANES - 2 * SWEEP_TALLY, 1)
    count, sum_u, sum_uu, h0_re, h0_im, hu_re, hu_im = (total[q:q + 1] for q in range(7))
    sum_v, sum_uv, hv_re, hv_im = (once[q:q + 1] for q in (0, 1, 3, 4))
    sum_vv = twice[0:1]
    floored = jnp.maximum(count, 1.0)
    mean_u = sum_u / floored
    mean_v = sum_v / floored
    guu = sum_uu - 2.0 * mean_u * sum_u + mean_u * mean_u * count
    guv = sum_uv - mean_u * sum_v - mean_v * sum_u + mean_u * mean_v * count
    gvv = sum_vv - 2.0 * mean_v * sum_v + mean_v * mean_v * count
    ridge = 0.001 * count + 1.0
    diag_u = guu + ridge
    diag_v = gvv + ridge
    inverse = 1.0 / (diag_u * diag_v - guv * guv)
    base = 1.0 / (count + ridge)
    out = []
    slopes_u, slopes_v = [], []
    for h0, hu, hv in ((h0_re, hu_re, hv_re), (h0_im, hu_im, hv_im)):
        hu = hu - mean_u * h0
        hv = hv - mean_v * h0
        out.append(h0 * base)
        slopes_u.append((diag_v * hu - guv * hv) * inverse)
        slopes_v.append((diag_u * hv - guv * hu) * inverse)
    entries = out + slopes_u + slopes_v + [mean_u, mean_v]
    stacked = jnp.zeros((LANES, LANES), F32)
    place = row_of((LANES, LANES))
    for i, entry in enumerate(entries):
        stacked = jnp.where(place == i, entry, stacked)
    stacked = jnp.where(lane_of((LANES, LANES)) < SWEEP_TALLY, stacked, 0.0)
    coefs[...] = lax.dot_general(
        membership[0], stacked, (((1,), (1,)), ((), ())), preferred_element_type=F32, precision=EXACT
    )


def ramp_kernel(count_rows, count_cols, gamma, size, coefs, deramped, coherence, out, sem):
    _, rows, cols = gamma.shape
    my_row = lax.axis_index("rows")
    my_col = lax.axis_index("cols")
    lane = lane_of((8, LANES))
    across_first = ((my_col * cols + lane).astype(F32) + 0.5) * (2.0 / (cols * count_cols)) - 1.0
    chunk = 16
    copies = [pltpu.make_async_copy(size, coherence, sem.at[0])]
    copies[0].start()
    for low in range(0, rows, chunk):
        @pl.loop(low // 8, (low + chunk) // 8)
        def _(group):
            start = pl.multiple_of(group * 8, 8)
            here = pl.ds(start, 8)
            line = coefs[here, :]
            along = ((my_row * rows + start + row_of((8, LANES))).astype(F32) + 0.5) * (
                2.0 / (rows * count_rows)
            ) - 1.0
            wide = [jnp.broadcast_to(line[:, q:q + 1], (8, LANES)) for q in range(8)]
            along = along - wide[7]
            base_re = wide[0] + wide[4] * along
            base_im = wide[1] + wide[5] * along
            centred = across_first - wide[6]
            for j in range(cols // LANES):
                there = pl.ds(j * LANES, LANES)
                du = centred + j * (LANES * 2.0 / (cols * count_cols))
                model_re = base_re + wide[2] * du
                model_im = base_im + wide[3] * du
                real, imag = gamma[0, here, there], gamma[1, here, there]
                out[0, here, there] = real * model_re + imag * model_im
                out[1, here, there] = imag * model_re - real * model_im

        here = pl.ds(low, chunk)
        copy = pltpu.make_async_copy(out.at[:, here, :], deramped.at[:, here, :], sem.at[len(copies)])
        copy.start()
        copies.append(copy)
    for copy in copies:
        copy.wait()


def on_device(count_rows, count_cols, lead, trail, flags, sweep):
    rows, cols = flags.shape
    tall = rows + 2 * HALO
    wide = 2 * LANES
    tiles, between = cols // wide, rows - 2 * HALO
    vmem = pl.BlockSpec(memory_space=pltpu.VMEM)
    hbm = pl.BlockSpec(memory_space=pl.ANY)
    dma = pltpu.SemaphoreType.DMA
    V = pltpu.VMEM
    gamma, size, coefs = pl.pallas_call(
        functools.partial(gamma_kernel, count_rows, count_cols),
        out_shape=(V((2, rows, cols), F32), V((rows, cols), F32), V((rows, LANES), F32)),
        in_specs=[hbm, hbm, hbm, hbm],
        out_specs=(vmem, vmem, vmem),
        scratch_shapes=[
            V((2, rows, cols), F32), V((2, rows, cols), F32), V((rows, cols), jnp.int32), V((1, rows), jnp.int32),
            V((4, 2 * rows, cols), BF16),
            V((3, HALO, cols), F32), V((3, HALO, cols), F32), V((3, HALO, cols), F32), V((3, HALO, cols), F32),
            V((rows, LANES), F32), V((rows, LANES), F32), V((tall, LANES), F32), V((tall, LANES), F32),
            V((rows, 2 * LANES), F32), V((2 * HALO, 2 * LANES), F32), V((2 * rows, 2 * LANES), BF16), V((4 * HALO, 2 * LANES), BF16),
            V((rows, 2 * rows), BF16), V((2 * HALO, 4 * HALO), BF16),
            V((4, 4 * HALO, cols), BF16), V((wide, wide), BF16), V((wide, wide), BF16),
            V((tiles, 4, between, wide), BF16), V((tiles, 4, between, wide), BF16),
            V((tiles, 4, between, wide), BF16), V((tiles, 4, between, wide), F32),
            V((4, 2 * HALO, cols), F32),
            V((tiles, 4, 2 * HALO, wide), BF16), V((tiles, 4, 2 * HALO, wide), BF16),
            V((tiles, 4, 2 * HALO, wide), BF16), V((tiles, 4, 2 * HALO, wide), F32),
            V((7, between, LANES), F32), V((7, 2 * HALO, LANES), F32),
            V((rows, LANES), F32), V((2, LANES, rows), F32),
            V((4, LANES), F32), V((3, 4, LANES), F32), V((4, LANES), F32), V((2 * REACH, 4, LANES), F32),
            dma((64,)), dma((2 * PARTS,)), dma((2 * PARTS,)), dma((6,)), dma((6,)), dma((3,)), dma((3,)),
            dma((2 * REACH,)), dma((2 * REACH,)), pltpu.SemaphoreType.REGULAR((3,)),
        ],
        compiler_params=pltpu.CompilerParams(
            collective_id=0, has_side_effects=True, vmem_limit_bytes=63_000_000
        ),
        name="coherence",
    )(lead, trail, flags, sweep.reshape(1, rows))
    return pl.pallas_call(
        functools.partial(ramp_kernel, count_rows, count_cols),
        out_shape=(
            jax.ShapeDtypeStruct((2, rows, cols), F32),
            jax.ShapeDtypeStruct((rows, cols), F32),
        ),
        in_specs=[vmem, vmem, vmem],
        out_specs=(hbm, hbm),
        scratch_shapes=[V((2, rows, cols), F32), dma((9,))],
        compiler_params=pltpu.CompilerParams(vmem_limit_bytes=16 * 1024 * 1024),
        name="ramp",
    )(gamma, size, coefs)


def solution(mesh):
    in_specs = (P(None, "rows", "cols"), P(None, "rows", "cols"), P("rows", "cols"), P("rows"))
    out_specs = (P(None, "rows", "cols"), P("rows", "cols"))
    body = functools.partial(on_device, mesh.shape["rows"], mesh.shape["cols"])
    return jax.shard_map(body, mesh=mesh, in_specs=in_specs, out_specs=out_specs, check_vma=False)
```

time: 32.9 us -> 29.9 us (0.909)
  Pallas kernels: 32.2 us -> 29.1 us
    pallas_call x1, Pallas kernels: 29.6 us -> 26.7 us  [on_device(): pl.pallas_call(functools.partial(gamma_kernel, count_rows, count_cols), o...]
where the time goes in v3:
time: 29.9 us; the launch traced here: 29.8 us
  Pallas kernels  29.1 us (97%)
  between operations  0.64 us (2%)
    pallas_call x1, Pallas kernels, on_device(): pl.pallas_call(functools.partial(gamma_kernel, count_rows, count_cols), o...  26.7 us
    pallas_call x1, Pallas kernels, on_device(): pl.pallas_call(functools.partial(ramp_kernel, count_rows, count_cols), ou...  2.43 us

profile of v3, /device:TPU:1, one launch (start us, length us, event | category | flops | bytes accessed | tf_op | source)
XLA Modules:
  0.0 29.8 jit_solution(15477208274729810273)
XLA Ops:
  0.6 26.7 %coherence.1 = (f32[2,128,2048]{2,1,0:T(8,128)S(1)}, f32[128,2048]{1,0:T(8,128)S(1)}, f32[128,128]{1,0:T(8,128)S(1)}) custom-call(f32[2,128,2048]{2,1,0:T(8,128)} %lead.1, f32[2,128,2048]{2,1,0:T(8,128)} %trail.1, s32[128,2048]{1,0:T(8,128)} %flags.1, s32[1,128]{1,0:T(1,128)} %bitcast.1), custom_call_target="tpu_custom_call" | custom-call | tf_op jit(solution)/shard_map/coherence/pallas_call | solution.py:521
  27.4 2.4 %ramp.1 = (f32[2,128,2048]{2,1,0:T(8,128)}, f32[128,2048]{1,0:T(8,128)}) custom-call(f32[2,128,2048]{2,1,0:T(8,128)S(1)} %get-tuple-element.5.gamma, f32[128,2048]{1,0:T(8,128)S(1)} %get-tuple-element.6.size, f32[128,128]{1,0:T(8,128)S(1)} %get-tuple-element.7.coefs), custom_call_target="tpu_custom_call" | custom-call | tf_op jit(solution)/shard_map/ramp/pallas_call | solution.py:550

commit v4 on v3

--- a/solution.py
+++ b/solution.py
@@ -18,12 +18,20 @@
 MESH = pl.DeviceIdType.MESH
 F32 = jnp.float32
 BF16 = jnp.bfloat16
-EXACT = lax.Precision.HIGHEST
 
 
 def split_pair(x):
     high = x.astype(BF16)
     return high, (x - high.astype(F32)).astype(BF16)
+
+
+def split_three(x):
+    high, rest = x.astype(BF16), x - x.astype(BF16).astype(F32)
+    return high, rest.astype(BF16), (rest - rest.astype(BF16).astype(F32)).astype(BF16)
+
+
+def across_lanes(x, y):
+    return lax.dot_general(x, y, (((1,), (1,)), ((), ())), preferred_element_type=F32)
 
 
 def lane_of(shape):
@@ -38,7 +46,7 @@
     count_rows, count_cols,
     lead, trail, flags, sweep_in,
     gamma, size, coefs,
-    first, second, weight, sweep, planes, up_out, down_out, above, below, left_out, right_out, left_in, right_in,
+    first, second, weight, sweep, planes, up_out, down_out, above, below, side_out, side_in, corner_in,
     side_boxed, side_edge, side_planes, corner_planes, band, tri, halo_planes, across_box, across_join,
     high_in, low_in, join_in, box_in, own_edge, high_edge, low_edge, join_edge, box_edge,
     line_in, line_edge, sums, membership, table, from_cols, table_rows, from_rows,
@@ -59,21 +67,26 @@
         pl.semaphore_signal(sem, inc=1, device_id=where, device_id_type=MESH)
 
     barrier = pltpu.get_barrier_semaphore()
-    def exists(d_row):
-        return my_row >= -d_row if d_row < 0 else my_row < count_rows - d_row
-
-    def if_row(d_row, act):
-        if d_row:
-            pl.when(exists(d_row))(act)
-        else:
-            act()
-
-    def number(*d_rows):
-        return sum(exists(d).astype(jnp.int32) for d in d_rows)
-
-    for a in (-1, 0, 1):
-        for b in (-1, 0, 1) if a else (-1, 1, 2):
-            if_row(a, lambda a=a, b=b: signal(barrier, at(a, b)))
+    def exists(d_row, d_col=0):
+        here, count, d = (my_row, count_rows, d_row) if d_row else (my_col, count_cols, d_col)
+        return here >= -d if d < 0 else here < count - d
+
+    def if_there(d_row, d_col, act):
+        pl.when(exists(d_row, d_col))(act)
+
+    def tell(sem, distance, along_rows):
+        for d in (-distance, distance):
+            where = (d, 0) if along_rows else (0, d)
+            if_there(*where, lambda where=where: signal(sem, at(*where)))
+
+    def number(distance, along_rows):
+        return sum(exists(*((d, 0) if along_rows else (0, d))).astype(jnp.int32) for d in (-distance, distance))
+
+    def hear(sem, distance, along_rows):
+        pl.semaphore_wait(sem, number(distance, along_rows))
+
+    tell(barrier, 1, True)
+    tell(barrier, 1, False)
 
     loads = []
 
@@ -98,6 +111,9 @@
     inner = rows - HALO
     part = cols // PARTS
     edge_loads = []
+    sweep_load = pltpu.make_async_copy(sweep_in, sweep, load_sem.at[len(loads)])
+    sweep_load.start()
+    loads.append(sweep_load)
     for c in range(PARTS):
         right = (c + 1) * part - (LANES if c == PARTS - 1 else 0)
         edge_loads.append(load(0, HALO, c * part, right) + load(inner, rows, c * part, right))
@@ -105,9 +121,6 @@
             edge_loads[0] += load(0, HALO, cols - LANES, cols) + load(inner, rows, cols - LANES, cols)
     side_loads = load(HALO, inner, 0, LANES) + load(HALO, inner, cols - LANES, cols)
     step = (inner - HALO) // 3
-    sweep_load = pltpu.make_async_copy(sweep_in, sweep, load_sem.at[len(loads)])
-    sweep_load.start()
-    loads.append(sweep_load)
     main_loads = [load(HALO + i * step, HALO + (i + 1) * step, LANES, cols - LANES) for i in range(3)]
 
     lane = lane_of((8, LANES))
@@ -117,8 +130,10 @@
         here = (pl.ds(row, HALO), pl.ds(block * LANES, LANES))
         w = weight[here].astype(F32)
         real_a, imag_a = first[(0,) + here] * w, first[(1,) + here] * w
-        real_b, imag_b = second[(0,) + here] * w, second[(1,) + here] * w
+        real_b, imag_b = second[(0,) + here], second[(1,) + here]
+        power_b = (real_b * real_b + imag_b * imag_b) * w
         if sends is not None:
+            real_b, imag_b = real_b * w, imag_b * w
             top = jnp.maximum(jnp.abs(real_b), jnp.abs(imag_b))
             some = top > 0.0
             unit = 1.0 / jnp.where(some, top, 1.0)
@@ -133,7 +148,7 @@
             real_a * real_b + imag_a * imag_b,
             imag_a * real_b - real_a * imag_b,
             real_a * real_a + imag_a * imag_a,
-            real_b * real_b + imag_b * imag_b,
+            power_b,
         )
 
     def fill(row, sends=None, some=range(blocks)):
@@ -144,41 +159,54 @@
                 planes[p, pl.ds(row, HALO), here] = high
                 planes[p, pl.ds(rows + row, HALO), here] = low
 
-    def pack(row):
-        packed_left = jnp.zeros((HALO, LANES), F32)
-        packed_right = jnp.zeros((HALO, LANES), F32)
-        for p, x in enumerate(products(row, 0)):
+    groups = rows // HALO
+    slot = LANES // groups
+
+    def pack(group):
+        packed = [jnp.zeros((HALO, LANES), F32) for _ in range(2)]
+        for p, x in enumerate(products(group * HALO, 0)):
             x = jnp.where(lane16 < SIDE, x, 0.0)
-            packed_left += x if p == 0 else pltpu.roll(x, SIDE * p, 1)
-        for p, x in enumerate(products(row, blocks - 1)):
-            packed_right += pltpu.roll(jnp.where(lane16 >= LANES - SIDE, x, 0.0), SIDE * (p + 1), 1)
-        left_out[pl.ds(row, HALO), :] = packed_left
-        right_out[pl.ds(row, HALO), :] = packed_right
-
-    def send(source, target, send_sem, recv_sem, d_row, d_col):
+            packed[0] += x if p == 0 else pltpu.roll(x, SIDE * p, 1)
+        for p, x in enumerate(products(group * HALO, blocks - 1)):
+            packed[1] += pltpu.roll(jnp.where(lane16 >= LANES - SIDE, x, 0.0), SIDE * (p + 1), 1)
+        return packed
+
+    def at_slot(x, group):
+        return pltpu.roll(x, slot * group, 1) if group else x
+
+    def send(source, target, send_sem, recv_sem, d_row, d_col, ring=False):
         copy = pltpu.make_async_remote_copy(
             src_ref=source, dst_ref=target, send_sem=send_sem, recv_sem=recv_sem,
             device_id=at(d_row, d_col), device_id_type=MESH,
         )
-        if_row(d_row, copy.start)
-        return copy, d_row
+        if ring:
+            copy.start()
+        else:
+            if_there(d_row, d_col, copy.start)
+        return copy, d_row, d_col, ring
 
     def finish_send(sent):
-        copy, d_row = sent
-        if_row(-d_row, copy.wait_recv)
-        if_row(d_row, copy.wait_send)
+        copy, d_row, d_col, ring = sent
+        if ring:
+            copy.wait()
+        else:
+            if_there(-d_row, -d_col, copy.wait_recv)
+            if_there(d_row, d_col, copy.wait_send)
 
     @pl.when(my_row == 0)
     def _():
         above[...] = jnp.zeros_like(above)
-        for arrived in (left_in, right_in):
-            arrived[pl.ds(0, HALO), :] = jnp.zeros((HALO, LANES), F32)
+        corner_in[0] = jnp.zeros((2, HALO, LANES), F32)
 
     @pl.when(my_row == count_rows - 1)
     def _():
         below[...] = jnp.zeros_like(below)
-        for arrived in (left_in, right_in):
-            arrived[pl.ds(rows + HALO, HALO), :] = jnp.zeros((HALO, LANES), F32)
+        corner_in[1] = jnp.zeros((2, HALO, LANES), F32)
+
+    for side, missing in enumerate((my_col == 0, my_col == count_cols - 1)):
+        @pl.when(missing)
+        def _(side=side):
+            side_in[side] = jnp.zeros((HALO, LANES), F32)
 
     distances = [d for k in range(REACH, 0, -1) for d in (-k, k)]
     for i, d in enumerate(distances):
@@ -186,46 +214,7 @@
         def _(i=i):
             from_rows[i] = jnp.zeros((4, LANES), F32)
 
-    col_copies, corner_copies, row_copies = [], [], []
-
-    def send_side(copies, source, target, low, count, to, d_row, d_col):
-        i = len(col_copies) + len(corner_copies)
-        copies.append(
-            send(
-                source.at[pl.ds(low, count), :], target.at[pl.ds(to, count), :],
-                col_send.at[i], col_recv.at[i], d_row, d_col,
-            )
-        )
-
-    sides = ((left_out, right_in, -1), (right_out, left_in, 1))
-    for c in range(PARTS):
-        arrive(edge_loads[c])
-        if c == 0:
-            pack(0)
-            pack(inner)
-        some = range(c * part // LANES, (c + 1) * part // LANES)
-        fill(0, up_out, some)
-        fill(inner, down_out, some)
-        if c == 0:
-            pl.semaphore_wait(barrier, 3 + 3 * number(-1, 1))
-            for source, target, d_col in sides:
-                send_side(corner_copies, source, target, 0, HALO, rows + HALO, -1, d_col)
-                send_side(corner_copies, source, target, inner, HALO, 0, 1, d_col)
-        there = pl.ds(c * part, part)
-        row_copies.append([
-            send(
-                source.at[:, :, there], target.at[:, :, there],
-                row_send.at[2 * c + i], row_recv.at[2 * c + i], d_row, 0,
-            )
-            for i, (source, target, d_row) in enumerate(((up_out, below, -1), (down_out, above, 1)))
-        ])
-    arrive(side_loads)
-    for row in range(HALO, inner, HALO):
-        pack(row)
-    for source, target, d_col in sides:
-        send_side(col_copies, source, target, 0, rows, HALO, 0, d_col)
-    for d in (-1, 1):
-        if_row(d, lambda d=d: signal(token.at[0], at(d, 0)))
+    col_copies, row_copies = [], []
 
     box_row = row_of((rows, 2 * rows))
     box_col = lax.rem(lane_of((rows, 2 * rows)), rows) - box_row
@@ -248,6 +237,53 @@
     after = (from_lane < SIDE - 1) & (to_lane >= wide - SIDE + 1 + from_lane)
     across_join[...] = jnp.where(before | after, 1.0, 0.0).astype(BF16)
 
+    def fill_edges(c):
+        arrive(edge_loads[c])
+        some = range(c * part // LANES, (c + 1) * part // LANES)
+        fill(0, up_out, some)
+        fill(inner, down_out, some)
+
+    def send_edges(c):
+        there = pl.ds(c * part, part)
+        row_copies.append([
+            send(
+                source.at[:, :, there], target.at[:, :, there],
+                row_send.at[2 * c + i], row_recv.at[2 * c + i], d_row, 0,
+            )
+            for i, (source, target, d_row) in enumerate(((up_out, below, -1), (down_out, above, 1)))
+        ])
+
+    fill_edges(0)
+    ends = [pack(0), pack(groups - 1)]
+    fill_edges(1)
+    arrive(side_loads)
+    middle = [pack(group) for group in range(1, groups - 1)]
+    for side in range(2):
+        side_out[side] = sum(
+            (at_slot(x[side], group) for group, x in enumerate(middle + ends[1:], 1)), ends[0][side]
+        )
+    pl.semaphore_wait(barrier, number(1, True) + number(1, False))
+    send_edges(0)
+    send_edges(1)
+    for side, d_col in enumerate((-1, 1)):
+        col_copies.append(
+            send(side_out.at[side], side_in.at[1 - side], col_send.at[side], col_recv.at[side], 0, d_col)
+        )
+    for c in range(2, PARTS):
+        fill_edges(c)
+        send_edges(c)
+    tell(token.at[0], 1, True)
+    tell(token.at[3], 1, False)
+
+    sweep_load.wait()
+    along = ((my_row * rows + lane_of((LANES, rows))).astype(F32) + 0.5) * (2.0 / (rows * count_rows)) - 1.0
+    burst = row_of((LANES, rows))
+    power = burst // SWEEP_TALLY
+    chosen = jnp.where((burst - power * SWEEP_TALLY == sweep[...]) & (power < 3), 1.0, 0.0)
+    for i, x in enumerate(split_three(chosen * jnp.where(power == 0, 1.0, jnp.where(power == 1, along, along * along)))):
+        membership[i] = x
+    membership[3] = jnp.transpose(jnp.where(burst == sweep[...], 1.0, 0.0)).astype(BF16)
+
     for i, copies in enumerate(main_loads):
         arrive(copies)
 
@@ -265,14 +301,6 @@
             low_in[n, p] = low
             own_edge[p, pl.ds(0, HALO), there] = box[:HALO]
             own_edge[p, pl.ds(HALO, HALO), there] = box[inner:]
-
-    sweep_load.wait()
-    along = ((my_row * rows + lane_of((LANES, rows))).astype(F32) + 0.5) * (2.0 / (rows * count_rows)) - 1.0
-    burst = row_of((LANES, rows))
-    power = burst // SWEEP_TALLY
-    chosen = jnp.where((burst - power * SWEEP_TALLY == sweep[...]) & (power < 3), 1.0, 0.0)
-    membership[1] = chosen * jnp.where(power == 0, 1.0, jnp.where(power == 1, along, along * along))
-    membership[0] = jnp.transpose(jnp.where(burst == sweep[...], 1.0, 0.0))
 
     def join(high_ref, low_ref, join_ref, count, n, packed):
         first_half = lane_of((count, LANES)) < LANES // 2
@@ -337,44 +365,36 @@
 
     run_inner(list(range(1, tiles - 1)), 1)
 
-    pl.semaphore_wait(token.at[0], number(-1, 1))
-    for d in (-2, 2):
-        if_row(d, lambda d=d: signal(token.at[1], at(d, 0)))
+    hear(token.at[0], 1, True)
+    tell(token.at[1], 2, True)
+    hear(token.at[3], 1, False)
+    tell(token.at[4], 2, False)
 
     for sent in col_copies:
         finish_send(sent)
+    corner_copies = [
+        send(side_in, corner_in.at[1 - k], col_send.at[2 + k], col_recv.at[2 + k], d_row, 0)
+        for k, d_row in enumerate((-1, 1))
+    ]
     side_exists = [jnp.where(my_col > 0, 1.0, 0.0), jnp.where(my_col < count_cols - 1, 1.0, 0.0)]
-    for i, arrived in enumerate((left_in, right_in)):
+    for i in range(2):
         there = pl.ds(i * LANES, LANES)
-        high, low = split_pair(arrived[pl.ds(HALO, rows), :] * side_exists[i])
-        side_planes[pl.ds(0, rows), there] = high
-        side_planes[pl.ds(rows, rows), there] = low
+        arrived = side_in[i] * side_exists[i]
+        for group in range(groups):
+            high, low = split_pair(pltpu.roll(arrived, LANES - slot * group, 1) if group else arrived)
+            side_planes[pl.ds(group * HALO, HALO), there] = high
+            side_planes[pl.ds(rows + group * HALO, HALO), there] = low
     side_boxed[...] = jnp.dot(band[...], side_planes[...], preferred_element_type=F32)
     run_inner([0, tiles - 1], None, side_boxed[pl.ds(HALO, between), :])
     for at_row in range(0, between, 8):
         gather_lines(line_in, at_row, at_row + HALO)
 
-    for sent in corner_copies:
-        finish_send(sent)
-    for i, arrived in enumerate((left_in, right_in)):
-        there = pl.ds(i * LANES, LANES)
-        for k, to in enumerate((0, rows + HALO)):
-            high, low = split_pair(arrived[pl.ds(to, HALO), :] * side_exists[i])
-            corner_planes[pl.ds(2 * k * HALO, HALO), there] = high
-            corner_planes[pl.ds((2 * k + 1) * HALO, HALO), there] = low
-    side_edge[...] = jnp.dot(tri[...], corner_planes[...], preferred_element_type=F32) + jnp.concatenate(
-        [side_boxed[pl.ds(0, HALO), :], side_boxed[pl.ds(inner, HALO), :]], axis=0
-    )
-
-    ready = 0
-    for c in range(PARTS):
-        for sent in row_copies[c]:
-            finish_send(sent)
-        if c == 0:
-            pl.semaphore_wait(token.at[1], number(-2, 2))
-            for d in (-4, 4):
-                if_row(d, lambda d=d: signal(token.at[2], at(d, 0)))
-        here = pl.ds(c * part, part)
+    for group in ((0, 1), (2,), (3,)):
+        for c in group:
+            for sent in row_copies[c]:
+                finish_send(sent)
+        start, last = group[0] * part // wide, (group[-1] + 1) * part // wide
+        here = pl.ds(start * wide, (last - start) * wide)
         for i, arrived in enumerate((above, below)):
             turned_re, turned_im, length = (arrived[q, :, here] for q in range(3))
             arrived_planes = (
@@ -384,34 +404,47 @@
                 high, low = split_pair(x)
                 halo_planes[p, pl.ds(2 * i * HALO, HALO), here] = high
                 halo_planes[p, pl.ds((2 * i + 1) * HALO, HALO), here] = low
-        last = (c + 1) * part // wide
-        for n in range(c * part // wide, last):
+        for n in range(start, last):
             there = pl.ds(n * wide, wide)
             for p in range(4):
                 extra = jnp.dot(tri[...], halo_planes[p, :, there], preferred_element_type=F32)
                 high, low = split_pair(own_edge[p, :, there] + extra)
                 high_edge[n, p] = high
                 low_edge[n, p] = low
-        until = last if last == tiles else last - 1
-        for n in range(ready, until):
-            join(high_edge, low_edge, join_edge, 2 * HALO, n, side_edge[...])
+        if last == tiles:
+            for sent in corner_copies:
+                finish_send(sent)
+            for i in range(2):
+                there = pl.ds(i * LANES, LANES)
+                for k in range(2):
+                    arrived = corner_in[k, i] * side_exists[i]
+                    high, low = split_pair(arrived if k else pltpu.roll(arrived, slot, 1))
+                    corner_planes[pl.ds(2 * k * HALO, HALO), there] = high
+                    corner_planes[pl.ds((2 * k + 1) * HALO, HALO), there] = low
+            side_edge[...] = jnp.dot(tri[...], corner_planes[...], preferred_element_type=F32) + jnp.concatenate(
+                [side_boxed[pl.ds(0, HALO), :], side_boxed[pl.ds(inner, HALO), :]], axis=0
+            )
+        ends_at = list(range(max(start - 1, 1), last - 1)) + ([tiles - 1, 0] if last == tiles else [])
+        for n in ends_at:
+            join(high_edge, low_edge, join_edge, 2 * HALO, n, side_edge[...] if last == tiles else None)
             box_across(high_edge, low_edge, join_edge, box_edge, 2 * HALO, n)
-        for n in range(ready, until):
+        for n in ends_at:
             for at_row in range(0, 2 * HALO, 8):
-                finish(box_edge, line_edge, n, at_row, at_row if at_row < HALO else at_row - HALO + inner, n == 0)
-        ready = until
+                finish(box_edge, line_edge, n, at_row, at_row if at_row < HALO else at_row - HALO + inner, n == 1)
+    hear(token.at[1], 2, True)
+    tell(token.at[2], 4, True)
     for at_row in range(0, 2 * HALO, 8):
         gather_lines(line_edge, at_row, at_row if at_row < HALO else at_row - HALO + inner)
 
-    full = lax.dot_general(
-        jnp.transpose(sums[...])[:8], membership[1], (((1,), (1,)), ((), ())), preferred_element_type=F32, precision=EXACT
-    )
+    lines = split_three(jnp.transpose(sums[...])[:16])
+    full = sum(across_lanes(lines[i], membership[j]) for i, j in ((2, 0), (0, 2), (1, 1), (1, 0), (0, 1), (0, 0)))[:8]
     table[...] = full[:4] + pltpu.roll(full[4:], LANES // 2, 1)
 
+    hear(token.at[4], 2, False)
     copies = [
-        send(table, from_cols.at[k - 1], ysend.at[k - 1], yrecv.at[k - 1], 0, k) for k in (2, 1, 3)
+        send(table, from_cols.at[k - 1], ysend.at[k - 1], yrecv.at[k - 1], 0, k, True) for k in (2, 1, 3)
     ]
-    pl.semaphore_wait(token.at[2], number(-4, 4))
+    hear(token.at[2], 4, True)
     for sent in copies:
         finish_send(sent)
     table_rows[...] = (table[...] + from_cols[0]) + (from_cols[1] + from_cols[2])
@@ -459,14 +492,13 @@
         slopes_u.append((diag_v * hu - guv * hv) * inverse)
         slopes_v.append((diag_u * hv - guv * hu) * inverse)
     entries = out + slopes_u + slopes_v + [mean_u, mean_v]
-    stacked = jnp.zeros((LANES, LANES), F32)
-    place = row_of((LANES, LANES))
+    stacked = jnp.zeros((16, LANES), F32)
+    place = row_of((16, LANES))
     for i, entry in enumerate(entries):
         stacked = jnp.where(place == i, entry, stacked)
-    stacked = jnp.where(lane_of((LANES, LANES)) < SWEEP_TALLY, stacked, 0.0)
-    coefs[...] = lax.dot_general(
-        membership[0], stacked, (((1,), (1,)), ((), ())), preferred_element_type=F32, precision=EXACT
-    )
+    stacked = jnp.where(lane_of((16, LANES)) < SWEEP_TALLY, stacked, 0.0)
+    high, middle, low = (across_lanes(membership[3], x) for x in split_three(stacked))
+    coefs[...] = high + middle + low
 
 
 def ramp_kernel(count_rows, count_cols, gamma, size, coefs, deramped, coherence, out, sem):
@@ -511,7 +543,6 @@
 
 def on_device(count_rows, count_cols, lead, trail, flags, sweep):
     rows, cols = flags.shape
-    tall = rows + 2 * HALO
     wide = 2 * LANES
     tiles, between = cols // wide, rows - 2 * HALO
     vmem = pl.BlockSpec(memory_space=pltpu.VMEM)
@@ -520,14 +551,15 @@
     V = pltpu.VMEM
     gamma, size, coefs = pl.pallas_call(
         functools.partial(gamma_kernel, count_rows, count_cols),
-        out_shape=(V((2, rows, cols), F32), V((rows, cols), F32), V((rows, LANES), F32)),
+        out_shape=(V((2, rows, cols), F32), V((rows, cols), F32), V((rows, 16), F32)),
         in_specs=[hbm, hbm, hbm, hbm],
         out_specs=(vmem, vmem, vmem),
         scratch_shapes=[
             V((2, rows, cols), F32), V((2, rows, cols), F32), V((rows, cols), jnp.int32), V((1, rows), jnp.int32),
             V((4, 2 * rows, cols), BF16),
             V((3, HALO, cols), F32), V((3, HALO, cols), F32), V((3, HALO, cols), F32), V((3, HALO, cols), F32),
-            V((rows, LANES), F32), V((rows, LANES), F32), V((tall, LANES), F32), V((tall, LANES), F32),
+            V((2, HALO, LANES), F32), V((2, HALO, LANES), F32),
+            V((2, 2, HALO, LANES), F32),
             V((rows, 2 * LANES), F32), V((2 * HALO, 2 * LANES), F32), V((2 * rows, 2 * LANES), BF16), V((4 * HALO, 2 * LANES), BF16),
             V((rows, 2 * rows), BF16), V((2 * HALO, 4 * HALO), BF16),
             V((4, 4 * HALO, cols), BF16), V((wide, wide), BF16), V((wide, wide), BF16),
@@ -537,10 +569,10 @@
             V((tiles, 4, 2 * HALO, wide), BF16), V((tiles, 4, 2 * HALO, wide), BF16),
             V((tiles, 4, 2 * HALO, wide), BF16), V((tiles, 4, 2 * HALO, wide), F32),
             V((7, between, LANES), F32), V((7, 2 * HALO, LANES), F32),
-            V((rows, LANES), F32), V((2, LANES, rows), F32),
+            V((rows, LANES), F32), V((4, LANES, rows), BF16),
             V((4, LANES), F32), V((3, 4, LANES), F32), V((4, LANES), F32), V((2 * REACH, 4, LANES), F32),
             dma((64,)), dma((2 * PARTS,)), dma((2 * PARTS,)), dma((6,)), dma((6,)), dma((3,)), dma((3,)),
-            dma((2 * REACH,)), dma((2 * REACH,)), pltpu.SemaphoreType.REGULAR((3,)),
+            dma((2 * REACH,)), dma((2 * REACH,)), pltpu.SemaphoreType.REGULAR((5,)),
         ],
         compiler_params=pltpu.CompilerParams(
             collective_id=0, has_side_effects=True, vmem_limit_bytes=63_000_000

time: 29.9 us -> 29.1 us (0.973)
  Pallas kernels: 29.1 us -> 28.4 us
    pallas_call x1, Pallas kernels: 26.7 us -> 26 us  [on_device(): pl.pallas_call(functools.partial(gamma_kernel, count_rows, count_cols), o...]
where the time goes in v4:
time: 29.1 us; the launch traced here: 29 us
  Pallas kernels  28.4 us (98%)
  between operations  0.64 us (2%)
    pallas_call x1, Pallas kernels, on_device(): pl.pallas_call(functools.partial(gamma_kernel, count_rows, count_cols), o...  26 us
    pallas_call x1, Pallas kernels, on_device(): pl.pallas_call(functools.partial(ramp_kernel, count_rows, count_cols), ou...  2.43 us

profile of v4, /device:TPU:1, one launch (start us, length us, event | category | flops | bytes accessed | tf_op | source)
XLA Modules:
  0.0 29.0 jit_solution(15468508589691816803)
XLA Ops:
  0.6 26.0 %coherence.1 = (f32[2,128,2048]{2,1,0:T(8,128)S(1)}, f32[128,2048]{1,0:T(8,128)S(1)}, f32[128,16]{1,0:T(8,128)S(1)}) custom-call(f32[2,128,2048]{2,1,0:T(8,128)} %lead.1, f32[2,128,2048]{2,1,0:T(8,128)} %trail.1, s32[128,2048]{1,0:T(8,128)} %flags.1, s32[1,128]{1,0:T(1,128)} %bitcast.1), custom_call_target="tpu_custom_call" | custom-call | tf_op jit(solution)/shard_map/coherence/pallas_call | solution.py:552
  26.6 2.4 %ramp.1 = (f32[2,128,2048]{2,1,0:T(8,128)}, f32[128,2048]{1,0:T(8,128)}) custom-call(f32[2,128,2048]{2,1,0:T(8,128)S(1)} %get-tuple-element.5.gamma, f32[128,2048]{1,0:T(8,128)S(1)} %get-tuple-element.6.size, f32[128,16]{1,0:T(8,128)S(1)} %get-tuple-element.7.coefs), custom_call_target="tpu_custom_call" | custom-call | tf_op jit(solution)/shard_map/ramp/pallas_call | solution.py:582

commit v5 on v4

--- a/solution.py
+++ b/solution.py
@@ -14,6 +14,7 @@
 SIDE = WIN_C // 2
 LANES = 128
 REACH = 8
+PEERS = 7
 PARTS = 4
 MESH = pl.DeviceIdType.MESH
 F32 = jnp.float32
@@ -208,13 +209,13 @@
         def _(side=side):
             side_in[side] = jnp.zeros((HALO, LANES), F32)
 
-    distances = [d for k in range(REACH, 0, -1) for d in (-k, k)]
+    distances = [d for k in range(REACH, 0, -2) for d in (-k, k)]
     for i, d in enumerate(distances):
         @pl.when(jnp.logical_not(exists(-d)))
         def _(i=i):
             from_rows[i] = jnp.zeros((4, LANES), F32)
 
-    col_copies, row_copies = [], []
+    row_copies = []
 
     box_row = row_of((rows, 2 * rows))
     box_col = lax.rem(lane_of((rows, 2 * rows)), rows) - box_row
@@ -254,21 +255,18 @@
         ])
 
     fill_edges(0)
-    ends = [pack(0), pack(groups - 1)]
-    fill_edges(1)
-    arrive(side_loads)
-    middle = [pack(group) for group in range(1, groups - 1)]
-    for side in range(2):
-        side_out[side] = sum(
-            (at_slot(x[side], group) for group, x in enumerate(middle + ends[1:], 1)), ends[0][side]
-        )
     pl.semaphore_wait(barrier, number(1, True) + number(1, False))
     send_edges(0)
+    fill_edges(1)
     send_edges(1)
-    for side, d_col in enumerate((-1, 1)):
-        col_copies.append(
-            send(side_out.at[side], side_in.at[1 - side], col_send.at[side], col_recv.at[side], 0, d_col)
-        )
+    arrive(side_loads)
+    lines = [pack(group) for group in range(groups)]
+    for side in range(2):
+        side_out[side] = sum((at_slot(x[side], group) for group, x in enumerate(lines[1:], 1)), lines[0][side])
+    col_copies = [
+        send(side_out.at[side], side_in.at[1 - side], col_send.at[side], col_recv.at[side], 0, d_col)
+        for side, d_col in enumerate((-1, 1))
+    ]
     for c in range(2, PARTS):
         fill_edges(c)
         send_edges(c)
@@ -363,19 +361,19 @@
                     finish(box_in, line_in, waiting, at_row, at_row + HALO, waiting == fresh_at)
             waiting = n
 
-    run_inner(list(range(1, tiles - 1)), 1)
-
-    hear(token.at[0], 1, True)
-    tell(token.at[1], 2, True)
-    hear(token.at[3], 1, False)
-    tell(token.at[4], 2, False)
-
     for sent in col_copies:
         finish_send(sent)
     corner_copies = [
         send(side_in, corner_in.at[1 - k], col_send.at[2 + k], col_recv.at[2 + k], d_row, 0)
         for k, d_row in enumerate((-1, 1))
     ]
+    run_inner(list(range(1, tiles - 1)), 1)
+
+    hear(token.at[0], 1, True)
+    tell(token.at[1], 2, True)
+    hear(token.at[3], 1, False)
+    tell(token.at[4], 2, False)
+
     side_exists = [jnp.where(my_col > 0, 1.0, 0.0), jnp.where(my_col < count_cols - 1, 1.0, 0.0)]
     for i in range(2):
         there = pl.ds(i * LANES, LANES)
@@ -431,8 +429,6 @@
         for n in ends_at:
             for at_row in range(0, 2 * HALO, 8):
                 finish(box_edge, line_edge, n, at_row, at_row if at_row < HALO else at_row - HALO + inner, n == 1)
-    hear(token.at[1], 2, True)
-    tell(token.at[2], 4, True)
     for at_row in range(0, 2 * HALO, 8):
         gather_lines(line_edge, at_row, at_row if at_row < HALO else at_row - HALO + inner)
 
@@ -441,13 +437,17 @@
     table[...] = full[:4] + pltpu.roll(full[4:], LANES // 2, 1)
 
     hear(token.at[4], 2, False)
+    partner = 1 - 2 * lax.rem(my_row, 2)
     copies = [
-        send(table, from_cols.at[k - 1], ysend.at[k - 1], yrecv.at[k - 1], 0, k, True) for k in (2, 1, 3)
+        send(table, from_cols.at[i], ysend.at[i], yrecv.at[i], partner if other else 0, k, True)
+        for i, (other, k) in enumerate(((1, 2), (0, 2), (1, 1), (1, 3), (0, 1), (0, 3), (1, 0)))
     ]
+    hear(token.at[1], 2, True)
+    tell(token.at[2], 4, True)
     hear(token.at[2], 4, True)
     for sent in copies:
         finish_send(sent)
-    table_rows[...] = (table[...] + from_cols[0]) + (from_cols[1] + from_cols[2])
+    table_rows[...] = sum((from_cols[i] for i in range(PEERS)), table[...])
     copies = [
         send(table_rows, from_rows.at[i], rsend.at[i], rrecv.at[i], d, 0) for i, d in enumerate(distances)
     ]
@@ -570,9 +570,9 @@
             V((tiles, 4, 2 * HALO, wide), BF16), V((tiles, 4, 2 * HALO, wide), F32),
             V((7, between, LANES), F32), V((7, 2 * HALO, LANES), F32),
             V((rows, LANES), F32), V((4, LANES, rows), BF16),
-            V((4, LANES), F32), V((3, 4, LANES), F32), V((4, LANES), F32), V((2 * REACH, 4, LANES), F32),
-            dma((64,)), dma((2 * PARTS,)), dma((2 * PARTS,)), dma((6,)), dma((6,)), dma((3,)), dma((3,)),
-            dma((2 * REACH,)), dma((2 * REACH,)), pltpu.SemaphoreType.REGULAR((5,)),
+            V((4, LANES), F32), V((PEERS, 4, LANES), F32), V((4, LANES), F32), V((REACH, 4, LANES), F32),
+            dma((64,)), dma((2 * PARTS,)), dma((2 * PARTS,)), dma((4,)), dma((4,)), dma((PEERS,)), dma((PEERS,)),
+            dma((REACH,)), dma((REACH,)), pltpu.SemaphoreType.REGULAR((5,)),
         ],
         compiler_params=pltpu.CompilerParams(
             collective_id=0, has_side_effects=True, vmem_limit_bytes=63_000_000

time: 29.1 us -> 28.2 us (0.969)
  Pallas kernels: 28.4 us -> 27.4 us
    pallas_call x1, Pallas kernels: 26 us -> 24.9 us  [on_device(): pl.pallas_call(functools.partial(gamma_kernel, count_rows, count_cols), o...]
where the time goes in v5:
time: 28.2 us; the launch traced here: 28 us
  Pallas kernels  27.4 us (97%)
  between operations  0.64 us (2%)
    pallas_call x1, Pallas kernels, on_device(): pl.pallas_call(functools.partial(gamma_kernel, count_rows, count_cols), o...  24.9 us
    pallas_call x1, Pallas kernels, on_device(): pl.pallas_call(functools.partial(ramp_kernel, count_rows, count_cols), ou...  2.43 us

profile of v5, /device:TPU:1, one launch (start us, length us, event | category | flops | bytes accessed | tf_op | source)
XLA Modules:
  0.0 28.0 jit_solution(11834839887747408129)
XLA Ops:
  0.6 24.9 %coherence.1 = (f32[2,128,2048]{2,1,0:T(8,128)S(1)}, f32[128,2048]{1,0:T(8,128)S(1)}, f32[128,16]{1,0:T(8,128)S(1)}) custom-call(f32[2,128,2048]{2,1,0:T(8,128)} %lead.1, f32[2,128,2048]{2,1,0:T(8,128)} %trail.1, s32[128,2048]{1,0:T(8,128)} %flags.1, s32[1,128]{1,0:T(1,128)} %bitcast.1), custom_call_target="tpu_custom_call" | custom-call | tf_op jit(solution)/shard_map/coherence/pallas_call | solution.py:552
  25.6 2.4 %ramp.1 = (f32[2,128,2048]{2,1,0:T(8,128)}, f32[128,2048]{1,0:T(8,128)}) custom-call(f32[2,128,2048]{2,1,0:T(8,128)S(1)} %get-tuple-element.5.gamma, f32[128,2048]{1,0:T(8,128)S(1)} %get-tuple-element.6.size, f32[128,16]{1,0:T(8,128)S(1)} %get-tuple-element.7.coefs), custom_call_target="tpu_custom_call" | custom-call | tf_op jit(solution)/shard_map/ramp/pallas_call | solution.py:582

commit v6 on v5

--- a/solution.py
+++ b/solution.py
@@ -16,6 +16,7 @@
 REACH = 8
 PEERS = 7
 PARTS = 4
+TINY = 1.1754944e-38
 MESH = pl.DeviceIdType.MESH
 F32 = jnp.float32
 BF16 = jnp.bfloat16
@@ -136,7 +137,7 @@
         if sends is not None:
             real_b, imag_b = real_b * w, imag_b * w
             top = jnp.maximum(jnp.abs(real_b), jnp.abs(imag_b))
-            some = top > 0.0
+            some = top >= TINY
             unit = 1.0 / jnp.where(some, top, 1.0)
             x, y = jnp.where(some, real_b * unit, 1.0), imag_b * unit
             square = x * x + y * y
@@ -255,6 +256,14 @@
         ])
 
     fill_edges(0)
+    sweep_load.wait()
+    along = ((my_row * rows + lane_of((LANES, rows))).astype(F32) + 0.5) * (2.0 / (rows * count_rows)) - 1.0
+    burst = row_of((LANES, rows))
+    power = burst // SWEEP_TALLY
+    chosen = jnp.where((burst - power * SWEEP_TALLY == sweep[...]) & (power < 3), 1.0, 0.0)
+    for i, x in enumerate(split_three(chosen * jnp.where(power == 0, 1.0, jnp.where(power == 1, along, along * along)))):
+        membership[i] = x
+    membership[3] = jnp.transpose(jnp.where(burst == sweep[...], 1.0, 0.0)).astype(BF16)
     pl.semaphore_wait(barrier, number(1, True) + number(1, False))
     send_edges(0)
     fill_edges(1)
@@ -272,15 +281,6 @@
         send_edges(c)
     tell(token.at[0], 1, True)
     tell(token.at[3], 1, False)
-
-    sweep_load.wait()
-    along = ((my_row * rows + lane_of((LANES, rows))).astype(F32) + 0.5) * (2.0 / (rows * count_rows)) - 1.0
-    burst = row_of((LANES, rows))
-    power = burst // SWEEP_TALLY
-    chosen = jnp.where((burst - power * SWEEP_TALLY == sweep[...]) & (power < 3), 1.0, 0.0)
-    for i, x in enumerate(split_three(chosen * jnp.where(power == 0, 1.0, jnp.where(power == 1, along, along * along)))):
-        membership[i] = x
-    membership[3] = jnp.transpose(jnp.where(burst == sweep[...], 1.0, 0.0)).astype(BF16)
 
     for i, copies in enumerate(main_loads):
         arrive(copies)

time: 28.2 us -> 28.2 us (level)
  no operation moved by 1% of the time
where the time goes in v6:
time: 28.2 us; the launch traced here: 28 us
  Pallas kernels  27.4 us (97%)
  between operations  0.64 us (2%)
    pallas_call x1, Pallas kernels, on_device(): pl.pallas_call(functools.partial(gamma_kernel, count_rows, count_cols), o...  24.9 us
    pallas_call x1, Pallas kernels, on_device(): pl.pallas_call(functools.partial(ramp_kernel, count_rows, count_cols), ou...  2.43 us

profile of v6, /device:TPU:1, one launch (start us, length us, event | category | flops | bytes accessed | tf_op | source)
XLA Modules:
  0.0 28.0 jit_solution(11036026218842194734)
XLA Ops:
  0.6 24.9 %coherence.1 = (f32[2,128,2048]{2,1,0:T(8,128)S(1)}, f32[128,2048]{1,0:T(8,128)S(1)}, f32[128,16]{1,0:T(8,128)S(1)}) custom-call(f32[2,128,2048]{2,1,0:T(8,128)} %lead.1, f32[2,128,2048]{2,1,0:T(8,128)} %trail.1, s32[128,2048]{1,0:T(8,128)} %flags.1, s32[1,128]{1,0:T(1,128)} %bitcast.1), custom_call_target="tpu_custom_call" | custom-call | tf_op jit(solution)/shard_map/coherence/pallas_call | solution.py:552
  25.6 2.4 %ramp.1 = (f32[2,128,2048]{2,1,0:T(8,128)}, f32[128,2048]{1,0:T(8,128)}) custom-call(f32[2,128,2048]{2,1,0:T(8,128)S(1)} %get-tuple-element.5.gamma, f32[128,2048]{1,0:T(8,128)S(1)} %get-tuple-element.6.size, f32[128,16]{1,0:T(8,128)S(1)} %get-tuple-element.7.coefs), custom_call_target="tpu_custom_call" | custom-call | tf_op jit(solution)/shard_map/ramp/pallas_call | solution.py:582
